TPU v7x, 32 devices: a whole 2x2x4 slice. The times are simulated.
32 devices in a mesh: patch: 8 (over z, y), dir: 4 (over x, core).
Axes of the slice: x: 2, y: 2, z: 4, core: 2. Of those that a mesh axis runs over, the one named last changes fastest.
Arguments:
- right_side: float32 [96, 192, 256], P('dir', 'patch'), may hold values from -6 to 6
- guess: float32 [96, 192, 256], P('dir', 'patch'), may hold values from -3 to 3
- mask_fine: int32 [96, 192, 2], P('dir', 'patch'), may hold values 0 or 1
- mask_next: int32 [48, 96, 1], P('dir', 'patch'), may hold values 0 or 1
Outputs:
- solution: float32 [96, 192, 256], P('dir', 'patch')
All inputs are finite; a program needn't handle non-finite values. No bound on the sum of `mask_fine` or of `mask_next` on one device may be relied on, other than what follows from the above.
Results may differ from a plain program's by a relative error of at most 0.00005.
Values sent between devices are 32-bit elements; how exact they have to be, the bound alone decides.
A program may use at most 64 MiB of HBM per device.

v0:
```python
import functools

import jax
import jax.numpy as jnp
import numpy as np
from jax import lax
from jax.experimental import pallas as pl
from jax.experimental.pallas import tpu as pltpu
from jax.sharding import PartitionSpec as P

TILE = 128
SWEEPS = 3
LEVELS = 4
MASS = tuple(v / 5040 for v in (1, 120, 1191, 2416, 1191, 120, 1))
STIFF = tuple(v / 120 for v in (-1, -24, -15, 80, -15, -24, -1))
SUBDIV = (0.125, 0.5, 0.75, 0.5, 0.125)
OMEGA = 0.5
MESH = pl.DeviceIdType.MESH
WAYS = ((0, 1), (0, -1), (1, 0), (1, 1), (1, -1), (-1, 0), (-1, 1), (-1, -1))


def up8(n):
    return -(-n // 8) * 8


def band(n, size, coeffs):
    i, j = np.indices((size, size))
    out = np.zeros((size, size), np.float32)
    for k, c in enumerate(coeffs):
        out[(j - i + 3 == k) & (i < n) & (j < n)] = c
    return out


def subdivision(n, rows, columns):
    i, j = np.indices((rows, columns))
    out = np.zeros((rows, columns), np.float32)
    for k, c in enumerate(SUBDIV):
        out[(i - 2 * j + 2 == k) & (i < 2 * n) & (j < n)] = c
    return out


def weights(width):
    bands, moves = [], []
    for level in range(LEVELS):
        n = width >> level
        size = max(n, 128)
        mass = band(n, size, (1, 120, 1191, 2416, 1191, 120, 1))
        high = mass.astype(jnp.bfloat16)
        low = (mass - high.astype(np.float32)).astype(jnp.bfloat16)
        stiff = band(n, size, (-1, -24, -15, 80, -15, -24, -1)).astype(jnp.bfloat16)
        bands.append(np.stack([high, low, stiff]))
        if level + 1 < LEVELS:
            move = subdivision(n // 2, size, max(n // 2, 128))
            moves.append((move.astype(jnp.bfloat16), np.ascontiguousarray(move.T).astype(jnp.bfloat16)))
    return bands, moves


def parts(x):
    high = x.astype(jnp.bfloat16)
    return high, (x - high.astype(jnp.float32)).astype(jnp.bfloat16)


def mul(a, b):
    return jnp.dot(a, b, preferred_element_type=jnp.float32)


def taps(x, coeffs):
    sums = (x[0] + x[6], x[1] + x[5], x[2] + x[4], x[3])
    total = coeffs[3] * sums[3]
    for k in range(3):
        total = total + coeffs[k] * sums[k]
    return total


def kernel(sets, n_dir, n_patch, rs, guess, s0, s1, *refs):
    bands, refs = refs[:LEVELS], refs[LEVELS:]
    moves, refs = refs[: 2 * (LEVELS - 1)], refs[2 * (LEVELS - 1) :]
    out, refs = refs[0], refs[1:]
    bufs = []
    for _ in sets:
        bufs.append(refs[:6])
        refs = refs[6:]
    fields = []
    for level in range(LEVELS):
        fields.append(refs[:6])
        refs = refs[6:]
    send_sem, recv_sem = refs
    masks = (s0, s1, None, None)

    me_u, me_v = lax.axis_index("dir"), lax.axis_index("patch")
    has_down, has_up = me_u > 0, me_u < n_dir - 1

    def device(a, b):
        return {"dir": me_u + a, "patch": lax.rem(me_v + b + n_patch, n_patch)}

    def when_way(a, body):
        if a == 0:
            body()
        else:
            pl.when(has_up if a > 0 else has_down)(body)

    barrier = pltpu.get_barrier_semaphore()
    for step in (0, 1, -1):
        def greet():
            for a, b in WAYS:
                if a == step:
                    pl.semaphore_signal(barrier, inc=1, device_id=device(a, b), device_id_type=MESH)
        when_way(step, greet)

    for (nu, nv, nvp, w), (c, sl, sr, rl, rr, p) in zip(sets, bufs):
        p[:, nvp + 8 :, :] = jnp.zeros((nu + 6, 8, w), jnp.float32)
        for flag, at in ((me_u == 0, 0), (me_u == n_dir - 1, nu + 3)):
            @pl.when(flag)
            def _():
                c[:, at : at + 3] = jnp.zeros((2, 3, nvp, w), jnp.float32)
                rl[:, at : at + 3] = jnp.zeros((2, 3, 3, w), jnp.float32)
                rr[:, at : at + 3] = jnp.zeros((2, 3, 3, w), jnp.float32)

    inside = jnp.logical_and(has_down, has_up)
    pl.when(inside)(lambda: pl.semaphore_wait(barrier, 8))
    pl.when(jnp.logical_not(inside))(lambda: pl.semaphore_wait(barrier, 5))

    def exchange(which, x, number):
        nu, nv, nvp, w = sets[which]
        c, sl, sr, rl, rr, p = bufs[which]
        slot = lax.rem(number, 2)

        def stage(u, _):
            row = x[u]
            c[slot, u + 3] = row
            sl[slot, u] = row[0:3]
            sr[slot, u] = row[nv - 3 : nv]
            return 0

        lax.fori_loop(0, nu, stage, 0, unroll=min(nu, 4))

        def copy(index):
            a, b = WAYS[index]
            if b == 0:
                at, to = (nu, 0) if a > 0 else (3, nu + 3)
                src, dst = c.at[slot, at : at + 3], c.at[slot, to : to + 3]
            else:
                near, far = (sr, rl) if b > 0 else (sl, rr)
                if a == 0:
                    src, dst = near.at[slot], far.at[slot, 3 : nu + 3]
                else:
                    at, to = (nu - 3, 0) if a > 0 else (0, nu + 3)
                    src, dst = near.at[slot, at : at + 3], far.at[slot, to : to + 3]
            return pltpu.make_async_remote_copy(
                src_ref=src,
                dst_ref=dst,
                send_sem=send_sem.at[slot, index],
                recv_sem=recv_sem.at[slot, index],
                device_id=device(a, b),
                device_id_type=MESH,
            )

        for step in (1, -1, 0):
            def start():
                for index, (a, b) in enumerate(WAYS):
                    if a == step:
                        copy(index).start()
            when_way(step, start)
        for step in (0, 1, -1):
            def finish():
                for index, (a, b) in enumerate(WAYS):
                    if a == step:
                        copy(index).wait_send()
                    if a == -step:
                        copy(index).wait_recv()
            when_way(step, finish)

        def gather(u, _):
            p[u, 8 : 8 + nvp] = c[slot, u]
            p[u, 5:8] = rl[slot, u]
            p[u, 8 + nv : 11 + nv] = rr[slot, u]
            return 0

        lax.fori_loop(0, nu + 6, gather, 0, unroll=6 if nu % 6 == 0 else 3)

    def chunked(which, body):
        nu, nv, nvp, w = sets[which]
        size = nu
        while size * nvp > 192 and size % 2 == 0:
            size //= 2
        if size == nu:
            body(0, nu)
        else:
            lax.fori_loop(0, nu // size, lambda i, _: (body(i * size, size), 0)[1], 0)

    def operate(level, x, number, use):
        which = set_of[level]
        nu, nv, nvp, w = sets[which]
        p = bufs[which][5]
        load, field, pu, ku, g, h = fields[level]
        exchange(which, x, number)

        def sublanes(u, _):
            t = [p[u, 5 + k : 5 + k + nvp, :] for k in range(7)]
            pu[u] = taps(t, [v / 5040 for v in MASS])
            ku[u] = taps(t, [v / 5040 for v in STIFF])
            return 0

        lax.fori_loop(0, nu + 6, sublanes, 0, unroll=6 if nu % 6 == 0 else 3)

        def leading(u, _):
            a = [pu[u + k] for k in range(7)]
            b = [ku[u + k] for k in range(7)]
            g[u] = taps(a, STIFF) + taps(b, MASS)
            h[u] = taps(a, [v * 42 for v in MASS])
            return 0

        lax.fori_loop(0, nu, leading, 0, unroll=4 if nu % 4 == 0 else 3)
        table = bands[level]

        def finish(u, size):
            g_high, g_low = parts(g[pl.ds(u, size)].reshape(size * nvp, w))
            h_high, h_low = parts(h[pl.ds(u, size)].reshape(size * nvp, w))
            value = mul(g_high, table[0]) + mul(g_low, table[0]) + mul(g_high, table[1])
            value = value + mul(h_high, table[2]) + mul(h_low, table[2])
            use(pl.ds(u, size), value.reshape(size, nvp, w))

        chunked(which, finish)

    def sweep(level, number):
        load, field = fields[level][:2]
        mask = masks[level]

        def use(at, value):
            update = (OMEGA / 2**level) * load[at] - OMEGA * value
            if mask is not None:
                update = update * mask[at]
            field[at] = field[at] + update

        operate(level, field, number, use)

    def sweeps(level, count, number):
        def body(i, _):
            sweep(level, number + i)
            return 0

        lax.fori_loop(0, count, body, 0)
        return number + count

    def descend(level, number):
        which = set_of[level]
        nu, nv, nvp, w = sets[which]
        load, field, pu, ku, g, h = fields[level]
        mask = masks[level]
        if level == 0:
            number = sweeps(level, SWEEPS, number)
        else:
            first = (OMEGA / 2**level) * load[...]
            field[...] = first if mask is None else first * mask[...]
            number = sweeps(level, SWEEPS - 1, number)
        if level + 1 < LEVELS:
            low_which = 1 if level == 0 else which
            low_p = bufs[low_which][5]
            down, up = moves[2 * level], moves[2 * level + 1]
            lanes = down.shape[1]

            def residual(at, value):
                r = load[at] - float(2**level) * value
                if mask is not None:
                    r = r * mask[at]
                size = r.shape[0]
                r_high, r_low = parts(r.reshape(size * nvp, w))
                n = mul(r_high, down[...]) + mul(r_low, down[...])
                g[at, :, 0:lanes] = n.reshape(size, nvp, lanes)

            operate(level, field, number, residual)
            number += 1
            exchange(low_which, g.at[:, :, 0:lanes], number)
            number += 1
            cu, cv, cvp, cw = sets[set_of[level + 1]]
            c_load, c_field = fields[level + 1][:2]
            c_p = bufs[set_of[level + 1]][5]
            c_load[...] = jnp.zeros((cu, cvp, cw), jnp.float32)
            for i in range(cu):
                total = None
                for k in range(5):
                    line = None
                    for m in range(5):
                        term = SUBDIV[m] * low_p[2 * i + k + 1, pl.ds(6 + m, cv, stride=2), :]
                        line = term if line is None else line + term
                    total = SUBDIV[k] * line if total is None else total + SUBDIV[k] * line
                c_load[i, 0:cv, :] = total
            number = descend(level + 1, number)
            exchange(set_of[level + 1], c_field, number)
            number += 1
            for u in range(nu):
                i = u // 2 + 3
                mix = ((i - 1, 0.125), (i, 0.75), (i + 1, 0.125)) if u % 2 == 0 else ((i, 0.5), (i + 1, 0.5))
                shifted = []
                for d in range(3):
                    total = None
                    for row, c in mix:
                        term = c * c_p[row, 7 + d : 7 + d + cv, :]
                        total = term if total is None else total + term
                    shifted.append(total)
                before, here, after = shifted
                spread[level][u, pl.ds(0, cv, stride=2), :] = 0.125 * (before + after) + 0.75 * here
                spread[level][u, pl.ds(1, cv, stride=2), :] = 0.5 * (here + after)

            def correct(at, size):
                at = pl.ds(at, size)
                y_high, y_low = parts(spread[level][at].reshape(size * nvp, lanes))
                y = (mul(y_high, up[...]) + mul(y_low, up[...])).reshape(size, nvp, w)
                if mask is not None:
                    y = y * mask[at]
                field[at] = field[at] + y

            chunked(which, correct)
        return sweeps(level, SWEEPS, number)

    set_of = [0, 2, 3, 4]
    spread = [bufs[1][0].at[0]] + [fields[level][3] for level in range(1, LEVELS)]
    load, field = fields[0][:2]
    load[...] = rs[...]
    field[...] = guess[...] * s0[...]
    descend(0, 0)
    out[...] = field[...]


def on_device(right_side, guess, mask_fine, mask_next):
    nu, nv, nw = right_side.shape
    sets = [(nu, nv, up8(nv), nw), (nu, nv, up8(nv), max(nw // 2, 128))]
    for level in range(1, LEVELS):
        sets.append((nu >> level, nv >> level, up8(nv >> level), max(nw >> level, 128)))
    sets = tuple(sets)
    bands, moves = weights(nw)
    s0 = jnp.repeat(mask_fine.astype(jnp.float32), TILE, axis=2)
    s1 = jnp.repeat(mask_next.astype(jnp.float32), TILE, axis=2)
    s1 = jnp.pad(s1, ((0, 0), (0, sets[2][2] - sets[2][1]), (0, sets[2][3] - s1.shape[2])))
    operands = [right_side, guess, s0, s1] + [jnp.asarray(b) for b in bands]
    operands += [jnp.asarray(m) for pair in moves for m in pair]
    scratch = []
    for u, v, vp, w in sets:
        scratch += [pltpu.VMEM((2, u + 6, vp, w), jnp.float32)]
        scratch += [pltpu.VMEM((2, u, 3, w), jnp.float32)] * 2
        scratch += [pltpu.VMEM((2, u + 6, 3, w), jnp.float32)] * 2
        scratch += [pltpu.VMEM((u + 6, vp + 16, w), jnp.float32)]
    for which in (0, 2, 3, 4):
        u, v, vp, w = sets[which]
        scratch += [pltpu.VMEM((u, vp, w), jnp.float32)] * 2
        scratch += [pltpu.VMEM((u + 6, vp, w), jnp.float32)] * 2
        scratch += [pltpu.VMEM((u, vp, w), jnp.float32)] * 2
    scratch += [pltpu.SemaphoreType.DMA((2, 8)), pltpu.SemaphoreType.DMA((2, 8))]
    vmem = pl.BlockSpec(memory_space=pltpu.VMEM)
    return pl.pallas_call(
        functools.partial(kernel, sets, lax.axis_size("dir"), lax.axis_size("patch")),
        out_shape=jax.ShapeDtypeStruct(right_side.shape, jnp.float32),
        in_specs=[vmem] * len(operands),
        out_specs=vmem,
        scratch_shapes=scratch,
        compiler_params=pltpu.CompilerParams(
            collective_id=0, has_side_effects=True, vmem_limit_bytes=60 * 2**20
        ),
        name="vcycle",
    )(*operands)


def solution(mesh):
    spec = P("dir", "patch", None)
    return jax.shard_map(
        on_device, mesh=mesh, in_specs=(spec,) * 4, out_specs=spec, check_vma=False
    )
```

profile of v0, /device:TPU:0, one launch (start us, length us, event | category | flops | bytes accessed | tf_op | source)
XLA Modules:
  0.0 182.4 jit_solution(9639189532458404602)
XLA Ops:
  0.0 0.0 copy-start
  0.0 0.7 convert_element_type.11
  0.7 0.0 copy-done
  0.8 0.1 reshape.8
  0.9 0.6 pad.4.s1
  1.5 0.2 copy.15
  1.7 0.8 broadcast_in_dim.4
  2.5 1.3 reshape.7.s0
  3.8 176.7 %vcycle.1 = f32[24,24,256]{2,1,0:T(8,128)} custom-call(f32[24,24,256]{2,1,0:T(8,128)} %rs.1, f32[24,24,256]{2,1,0:T(8,128)} %guess.1, f32[24,24,256]{2,1,0:T(8,128)} %reshape.7.s0, f32[12,16,128]{2,1,0:T(8,128)} %pad.4.s1, bf16[3,256,256]{2,1,0:T(8,128)(2,1)} %constant.23.clone.refs_0_, bf16[3,128,128]{2,1,0:T(8,128)(2,1)} %constant.24.clone.refs_1_, ...), custom_call_target="tpu_custom_call" | custom-call | tf_op jit(solution)/shard_map/vcycle/pallas_call | solution.py:350
  180.4 1.9 %copy.20 = f32[24,24,256]{2,1,0:T(8,128)} copy(f32[24,24,256]{2,1,0:T(8,128)} %vcycle.1) | data formatting | bytes 1179648
  (2 shorter events, 0.0 us)
Async XLA Ops:
  0.0 0.8 copy-start
where the time goes:
time: 183 us; the launch traced here: 182 us
  Pallas kernels  177 us (97%)
  local copies, waits for them, and re-layouts  4.96 us (3%)
    pallas_call x1, Pallas kernels, on_device(): pl.pallas_call(functools.partial(kernel, sets, lax.axis_size('dir'), lax....  177 us

commit v1 on v0

--- a/solution.py
+++ b/solution.py
@@ -72,20 +72,214 @@
     return total
 
 
+BASIS = (2496, 1176, 96)
+KAPPA = OMEGA * 42 / 5040.0**3
+
+
+def coarse_weights(width):
+    wide, narrow = width >> 2, width >> 3
+    tables = []
+    for n in (wide, narrow):
+        copies = np.eye(128 // n, dtype=np.float32)
+        five = band(n, n, (0, 96, 1176, 2496, 1176, 96, 0))
+        stiff = band(n, n, (-1, -24, -15, 80, -15, -24, -1))
+        tables.append(np.stack([np.kron(copies, five), np.kron(copies, stiff)]))
+    move = subdivision(narrow, wide, narrow)
+    halves = np.eye(128 // wide, dtype=np.float32)
+    down = np.kron(halves, np.concatenate([move, move], axis=1))
+    zero = np.zeros_like(move.T)
+    even = np.kron(halves, np.concatenate([move.T, zero], axis=0))
+    odd = np.kron(halves, np.concatenate([zero, move.T], axis=0))
+    tables.append(np.stack([down, even, odd]))
+    return [t.astype(jnp.bfloat16) for t in tables]
+
+
+def sums(x):
+    return x[3], x[2] + x[4], x[1] + x[5], x[0] + x[6]
+
+
+def five_taps(s):
+    return BASIS[0] * s[0] + BASIS[1] * s[1] + BASIS[2] * s[2]
+
+
+def stiff_taps(s):
+    return 80.0 * s[0] - 15.0 * s[1] - 24.0 * s[2] - s[3]
+
+
+def first_pass(x):
+    s = sums(x)
+    b, k = five_taps(s), stiff_taps(s)
+    d = b - 2.0 * k
+    return d, d + (b - k)
+
+
+def second_pass(d, e):
+    d, e = sums(d), sums(e)
+    g = five_taps(e) - (4912.0 * d[0] + 2367.0 * d[1] + 216.0 * d[2] + d[3])
+    q = five_taps(d) - stiff_taps(e)
+    return g, q
+
+
+def split_mul(x, table):
+    high, low = parts(x)
+    n = x.shape[0]
+    both = mul(jnp.concatenate([high, low], axis=0), table)
+    return both[:n] + both[n:]
+
+
+def last_pass(g, q, table):
+    return split_mul(g, table[0]) + split_mul(q, table[1])
+
+
+def rows_at_once(count, rows):
+    best = 1
+    for n in range(1, count + 1):
+        if count % n == 0 and n * rows <= 192:
+            best = n
+    return best
+
+
+def loop(count, body, unroll=1):
+    while count % unroll:
+        unroll -= 1
+    lax.fori_loop(0, count, lambda i, _: (body(i), 0)[1], 0, unroll=unroll)
+
+
+def apply_packed(x, d, e, table, at, base, rows, count, use):
+    def one(u):
+        d[u + 3], e[u + 3] = first_pass([x[at + u, base - 3 + k : base - 3 + k + rows, :] for k in range(7)])
+
+    loop(count, one, 3)
+    size = rows_at_once(count, rows)
+
+    def some(i):
+        u = i * size
+        gs, qs = [], []
+        for j in range(size):
+            g, q = second_pass([d[u + j + k] for k in range(7)], [e[u + j + k] for k in range(7)])
+            gs.append(g)
+            qs.append(q)
+        value = last_pass(jnp.concatenate(gs, axis=0), jnp.concatenate(qs, axis=0), table)
+        for j in range(size):
+            use(u + j, value[j * rows : (j + 1) * rows])
+
+    loop(count // size, some)
+
+
+def coarse_cycle(shape, load2, tables, refs):
+    nu, nh = shape
+    cu, nq = nu // 2, nh // 4
+    nqp = up8(nq)
+    x2, d2, e2, b2, t2, x3, f3, d3, e3, z3 = refs
+    edge = (x2.shape[0] - nu) // 2
+
+    def put2(u, new):
+        x2[edge + u, 8 : 8 + nh] = new
+        x2[edge + u, 0:8] = pltpu.roll(new[nh - 8 : nh], 64, 1)
+        x2[edge + u, 8 + nh : 16 + nh] = pltpu.roll(new[0:8], 64, 1)
+
+    def put3(u, new):
+        x3[u, 8 : 8 + nqp] = new
+        left, right = pltpu.roll(new, 32, 1), pltpu.roll(new[0:8], 96, 1)
+        x3[u, 5:8] = left[nq - 3 : nq]
+        x3[u, 8 + nq : 11 + nq] = right[0:3]
+
+    def smooth2():
+        def use(u, value):
+            put2(u, x2[edge + u, 8 : 8 + nh] + ((OMEGA / 4) * load2[u] - KAPPA * value))
+        apply_packed(x2, d2, e2, tables[0], edge, 8, nh, nu, use)
+
+    loop(nu, lambda u: put2(u, (OMEGA / 4) * load2[u]), 4)
+    loop(SWEEPS - 1, lambda i: smooth2())
+
+    size = rows_at_once(nu, nh)
+
+    def keep(u, value):
+        t2[u] = load2[u] - (8 * KAPPA) * value
+
+    apply_packed(x2, d2, e2, tables[0], edge, 8, nh, nu, keep)
+
+    def narrow(i):
+        at = pl.ds(i * size, size)
+        n = split_mul(t2[at].reshape(size * nh, 128), tables[2][0]).reshape(size, nh, 128)
+        b2[pl.ds(i * size + 2, size), 8 : 8 + nh] = n
+        for j in range(size):
+            b2[i * size + 2 + j, 0:8] = pltpu.roll(n[j, nh - 8 : nh], 64, 1)
+            b2[i * size + 2 + j, 8 + nh : 16 + nh] = pltpu.roll(n[j, 0:8], 64, 1)
+
+    loop(nu // size, narrow)
+    lane = lax.broadcasted_iota(jnp.int32, (nq, 128), 1)
+    first = lax.rem(lane // 32, 2) == 0
+
+    def restrict(i):
+        total = None
+        for k in range(5):
+            term = SUBDIV[k] * b2[2 * i + k]
+            total = term if total is None else total + term
+        z3[i] = total
+        lines = []
+        for start in (6, 6 + 2 * nq):
+            line = None
+            for m in range(5):
+                term = SUBDIV[m] * z3[i, pl.ds(start + m, nq, stride=2), :]
+                line = term if line is None else line + term
+            lines.append(line)
+        f3[i, 0:nq] = jnp.where(first, lines[0], lines[1])
+
+    loop(cu, restrict, 4)
+    loop(cu, lambda u: put3(u, (OMEGA / 8) * f3[u]), 4)
+
+    def smooth3(i):
+        def use(u, value):
+            put3(u, x3[u, 8 : 8 + nqp] + ((OMEGA / 8) * f3[u] - KAPPA * value))
+        apply_packed(x3, d3, e3, tables[1], 0, 8, nqp, cu, use)
+
+    loop(2 * SWEEPS - 1, smooth3)
+
+    nf = 2 * nq
+    for u in range(cu):
+        b, h, a = (x3[u, 7 + s : 7 + s + nq] for s in range(3))
+        b2[2 + u, pl.ds(0, nq, stride=2), :] = 0.125 * (b + a) + 0.75 * h
+        b2[2 + u, pl.ds(1, nq, stride=2), :] = 0.5 * (h + a)
+    fine = up8(nf)
+    for u in range(cu):
+        here = b2[2 + u, 0:fine]
+        after = b2[3 + u, 0:fine] if u + 1 < cu else jnp.zeros_like(here)
+        before = b2[1 + u, 0:fine] if u > 0 else jnp.zeros_like(here)
+        t2[2 * u, 0:fine] = 0.125 * (before + after) + 0.75 * here
+        t2[2 * u + 1, 0:fine] = 0.5 * (here + after)
+
+    def widen(i):
+        at = pl.ds(i * size, size)
+        z = t2[at, 0:fine].reshape(size * fine, 128)
+        y = (split_mul(z, tables[2][1]).reshape(size, fine, 128), split_mul(z, tables[2][2]).reshape(size, fine, 128))
+        for j in range(size):
+            u = edge + i * size + j
+            for s in range(2):
+                x2[u, 8 + s * nf : 8 + (s + 1) * nf] += y[s][j, 0:nf]
+            put2(i * size + j, x2[u, 8 : 8 + nh])
+
+    loop(nu // size, widen)
+    loop(SWEEPS, lambda i: smooth2())
+
+
 def kernel(sets, n_dir, n_patch, rs, guess, s0, s1, *refs):
-    bands, refs = refs[:LEVELS], refs[LEVELS:]
-    moves, refs = refs[: 2 * (LEVELS - 1)], refs[2 * (LEVELS - 1) :]
+    bands, refs = refs[:2], refs[2:]
+    moves, refs = refs[:4], refs[4:]
+    tables, refs = refs[:3], refs[3:]
     out, refs = refs[0], refs[1:]
     bufs = []
     for _ in sets:
         bufs.append(refs[:6])
         refs = refs[6:]
     fields = []
-    for level in range(LEVELS):
+    for level in range(2):
         fields.append(refs[:6])
         refs = refs[6:]
-    send_sem, recv_sem = refs
-    masks = (s0, s1, None, None)
+    c2, packed, slots, load2 = refs[:4]
+    coarse, refs = refs[4:14], refs[14:]
+    send_sem, recv_sem, all_send, all_recv = refs
+    masks = (s0, s1)
 
     me_u, me_v = lax.axis_index("dir"), lax.axis_index("patch")
     has_down, has_up = me_u > 0, me_u < n_dir - 1
@@ -99,13 +293,21 @@
         else:
             pl.when(has_up if a > 0 else has_down)(body)
 
+    n_all = n_dir * n_patch
+    me = me_u * n_patch + me_v
+
+    def place(flat):
+        return lax.div(flat, n_patch), lax.rem(flat, n_patch)
+
     barrier = pltpu.get_barrier_semaphore()
-    for step in (0, 1, -1):
-        def greet():
-            for a, b in WAYS:
-                if a == step:
-                    pl.semaphore_signal(barrier, inc=1, device_id=device(a, b), device_id_type=MESH)
-        when_way(step, greet)
+
+    def greet(i):
+        u, v = place(lax.rem(me + 1 + i, n_all))
+        pl.semaphore_signal(barrier, inc=1, device_id={"dir": u, "patch": v}, device_id_type=MESH)
+
+    loop(n_all - 1, greet)
+    for ref in (coarse[0], coarse[1], coarse[2], coarse[3], coarse[6], coarse[7], coarse[8]):
+        ref[...] = jnp.zeros_like(ref)
 
     for (nu, nv, nvp, w), (c, sl, sr, rl, rr, p) in zip(sets, bufs):
         p[:, nvp + 8 :, :] = jnp.zeros((nu + 6, 8, w), jnp.float32)
@@ -116,9 +318,7 @@
                 rl[:, at : at + 3] = jnp.zeros((2, 3, 3, w), jnp.float32)
                 rr[:, at : at + 3] = jnp.zeros((2, 3, 3, w), jnp.float32)
 
-    inside = jnp.logical_and(has_down, has_up)
-    pl.when(inside)(lambda: pl.semaphore_wait(barrier, 8))
-    pl.when(jnp.logical_not(inside))(lambda: pl.semaphore_wait(barrier, 5))
+    pl.semaphore_wait(barrier, n_all - 1)
 
     def exchange(which, x, number):
         nu, nv, nvp, w = sets[which]
@@ -253,7 +453,7 @@
             first = (OMEGA / 2**level) * load[...]
             field[...] = first if mask is None else first * mask[...]
             number = sweeps(level, SWEEPS - 1, number)
-        if level + 1 < LEVELS:
+        if True:
             low_which = 1 if level == 0 else which
             low_p = bufs[low_which][5]
             down, up = moves[2 * level], moves[2 * level + 1]
@@ -272,9 +472,16 @@
             number += 1
             exchange(low_which, g.at[:, :, 0:lanes], number)
             number += 1
-            cu, cv, cvp, cw = sets[set_of[level + 1]]
-            c_load, c_field = fields[level + 1][:2]
-            c_p = bufs[set_of[level + 1]][5]
+            if level == 0:
+                cu, cv, cvp, cw = sets[set_of[1]]
+                c_load, c_field = fields[1][:2]
+                c_p = bufs[set_of[1]][5]
+                corner = (3, 8)
+            else:
+                cu, cv, cvp, cw = nu // 2, nv // 2, up8(nv // 2), 128
+                c_load = c2
+                c_p = coarse[0]
+                corner = ((c_p.shape[0] - cu * n_dir) // 2 + me_u * cu, 8 + cv)
             c_load[...] = jnp.zeros((cu, cvp, cw), jnp.float32)
             for i in range(cu):
                 total = None
@@ -285,17 +492,21 @@
                         line = term if line is None else line + term
                     total = SUBDIV[k] * line if total is None else total + SUBDIV[k] * line
                 c_load[i, 0:cv, :] = total
-            number = descend(level + 1, number)
-            exchange(set_of[level + 1], c_field, number)
-            number += 1
+            if level == 0:
+                number = descend(1, number)
+                exchange(set_of[1], c_field, number)
+                number += 1
+            else:
+                gather_all(cu, cv)
+                coarse_cycle((cu * n_dir, cv * n_patch // 2), load2, tables, coarse)
             for u in range(nu):
-                i = u // 2 + 3
+                i = u // 2 + corner[0]
                 mix = ((i - 1, 0.125), (i, 0.75), (i + 1, 0.125)) if u % 2 == 0 else ((i, 0.5), (i + 1, 0.5))
                 shifted = []
                 for d in range(3):
                     total = None
                     for row, c in mix:
-                        term = c * c_p[row, 7 + d : 7 + d + cv, :]
+                        term = c * c_p[row, corner[1] - 1 + d : corner[1] - 1 + d + cv, :]
                         total = term if total is None else total + term
                     shifted.append(total)
                 before, here, after = shifted
@@ -313,8 +524,38 @@
             chunked(which, correct)
         return sweeps(level, SWEEPS, number)
 
-    set_of = [0, 2, 3, 4]
-    spread = [bufs[1][0].at[0]] + [fields[level][3] for level in range(1, LEVELS)]
+    def gather_all(cu, cv):
+        half = cu // 2
+        for j in range(half):
+            packed[j] = (c2[j] + pltpu.roll(c2[j + half], 64, 1))[0:cv]
+            slots[me_u, 1, j] = packed[j]
+
+        def copy(i, incoming):
+            flat = lax.rem(me + 1 + i, n_all) if not incoming else lax.rem(me + n_all - 1 - i, n_all)
+            u, v = place(flat)
+            source_u, source_v, target_v = (u, v, me_v) if incoming else (me_u, me_v, v)
+            return pltpu.make_async_remote_copy(
+                src_ref=packed,
+                dst_ref=slots.at[source_u, lax.rem(source_v - target_v + 1 + n_patch, n_patch)],
+                send_sem=all_send.at[i],
+                recv_sem=all_recv.at[i],
+                device_id={"dir": u, "patch": v},
+                device_id_type=MESH,
+            )
+
+        loop(n_all - 1, lambda i: copy(i, False).start())
+        loop(n_all - 1, lambda i: copy(i, False).wait_send())
+        loop(n_all - 1, lambda i: copy(i, True).wait_recv())
+        low = lax.broadcasted_iota(jnp.int32, (cv, 128), 1) < 64
+        for d in range(n_dir):
+            for k in range(n_patch // 2):
+                for j in range(half):
+                    a, b = slots[d, k, j], slots[d, k + n_patch // 2, j]
+                    load2[d * cu + j, k * cv : (k + 1) * cv] = jnp.where(low, a, pltpu.roll(b, 64, 1))
+                    load2[d * cu + half + j, k * cv : (k + 1) * cv] = jnp.where(low, pltpu.roll(a, 64, 1), b)
+
+    set_of = [0, 2]
+    spread = [bufs[1][0].at[0], fields[1][3]]
     load, field = fields[0][:2]
     load[...] = rs[...]
     field[...] = guess[...] * s0[...]
@@ -325,30 +566,51 @@
 def on_device(right_side, guess, mask_fine, mask_next):
     nu, nv, nw = right_side.shape
     sets = [(nu, nv, up8(nv), nw), (nu, nv, up8(nv), max(nw // 2, 128))]
-    for level in range(1, LEVELS):
-        sets.append((nu >> level, nv >> level, up8(nv >> level), max(nw >> level, 128)))
+    sets.append((nu >> 1, nv >> 1, up8(nv >> 1), max(nw >> 1, 128)))
     sets = tuple(sets)
     bands, moves = weights(nw)
     s0 = jnp.repeat(mask_fine.astype(jnp.float32), TILE, axis=2)
     s1 = jnp.repeat(mask_next.astype(jnp.float32), TILE, axis=2)
     s1 = jnp.pad(s1, ((0, 0), (0, sets[2][2] - sets[2][1]), (0, sets[2][3] - s1.shape[2])))
-    operands = [right_side, guess, s0, s1] + [jnp.asarray(b) for b in bands]
-    operands += [jnp.asarray(m) for pair in moves for m in pair]
+    operands = [right_side, guess, s0, s1] + [jnp.asarray(b) for b in bands[:2]]
+    operands += [jnp.asarray(m) for pair in moves[:2] for m in pair]
+    operands += [jnp.asarray(t) for t in coarse_weights(nw)]
+    n_dir, n_patch = lax.axis_size("dir"), lax.axis_size("patch")
+    cu, cv = nu >> 2, nv >> 2
+    gu, gh = cu * n_dir, cv * n_patch // 2
+    eu, eq = gu // 2, up8(gh // 4)
     scratch = []
     for u, v, vp, w in sets:
         scratch += [pltpu.VMEM((2, u + 6, vp, w), jnp.float32)]
         scratch += [pltpu.VMEM((2, u, 3, w), jnp.float32)] * 2
         scratch += [pltpu.VMEM((2, u + 6, 3, w), jnp.float32)] * 2
         scratch += [pltpu.VMEM((u + 6, vp + 16, w), jnp.float32)]
-    for which in (0, 2, 3, 4):
+    for which in (0, 2):
         u, v, vp, w = sets[which]
         scratch += [pltpu.VMEM((u, vp, w), jnp.float32)] * 2
         scratch += [pltpu.VMEM((u + 6, vp, w), jnp.float32)] * 2
         scratch += [pltpu.VMEM((u, vp, w), jnp.float32)] * 2
+    scratch += [
+        pltpu.VMEM((cu, up8(cv), 128), jnp.float32),
+        pltpu.VMEM((cu // 2, cv, 128), jnp.float32),
+        pltpu.VMEM((n_dir, n_patch, cu // 2, cv, 128), jnp.float32),
+        pltpu.VMEM((gu, gh, 128), jnp.float32),
+        pltpu.VMEM((gu + 18, gh + 16, 128), jnp.float32),
+        pltpu.VMEM((gu + 6, gh, 128), jnp.float32),
+        pltpu.VMEM((gu + 6, gh, 128), jnp.float32),
+        pltpu.VMEM((gu + 4, gh + 16, 128), jnp.float32),
+        pltpu.VMEM((gu, gh, 128), jnp.float32),
+        pltpu.VMEM((eu, eq + 16, 128), jnp.float32),
+        pltpu.VMEM((eu, eq, 128), jnp.float32),
+        pltpu.VMEM((eu + 6, eq, 128), jnp.float32),
+        pltpu.VMEM((eu + 6, eq, 128), jnp.float32),
+        pltpu.VMEM((eu, gh + 16, 128), jnp.float32),
+    ]
     scratch += [pltpu.SemaphoreType.DMA((2, 8)), pltpu.SemaphoreType.DMA((2, 8))]
+    scratch += [pltpu.SemaphoreType.DMA((n_dir * n_patch - 1,))] * 2
     vmem = pl.BlockSpec(memory_space=pltpu.VMEM)
     return pl.pallas_call(
-        functools.partial(kernel, sets, lax.axis_size("dir"), lax.axis_size("patch")),
+        functools.partial(kernel, sets, n_dir, n_patch),
         out_shape=jax.ShapeDtypeStruct(right_side.shape, jnp.float32),
         in_specs=[vmem] * len(operands),
         out_specs=vmem,

time: 183 us -> 143 us (0.78)
  Pallas kernels: 177 us -> 137 us
    pallas_call x1, Pallas kernels: 177 us -> 137 us  [on_device(): pl.pallas_call(functools.partial(kernel, sets, n_dir, n_patch), out_shape...]
where the time goes in v1:
time: 143 us
  Pallas kernels  137 us (96%)
  local copies, waits for them, and re-layouts  4.96 us (3%)
    pallas_call x1, Pallas kernels, on_device(): pl.pallas_call(functools.partial(kernel, sets, n_dir, n_patch), out_shape...  137 us

profile of v1, /device:TPU:0, one launch (start us, length us, event | category | flops | bytes accessed | tf_op | source)
XLA Modules:
  0.0 143.1 jit_solution(13777727539253264860)
XLA Ops:
  0.0 0.0 copy-start
  0.0 0.7 convert_element_type.11
  0.7 0.0 copy-done
  0.8 0.1 reshape.8
  0.9 0.6 pad.4.s1
  1.5 0.2 copy.14
  1.7 0.8 broadcast_in_dim.4
  2.5 1.3 reshape.7.s0
  3.8 137.4 %vcycle.1 = f32[24,24,256]{2,1,0:T(8,128)} custom-call(f32[24,24,256]{2,1,0:T(8,128)} %rs.1, f32[24,24,256]{2,1,0:T(8,128)} %guess.1, f32[24,24,256]{2,1,0:T(8,128)} %reshape.7.s0, f32[12,16,128]{2,1,0:T(8,128)} %pad.4.s1, bf16[3,256,256]{2,1,0:T(8,128)(2,1)} %constant.21.clone.refs_0_, bf16[3,128,128]{2,1,0:T(8,128)(2,1)} %constant.22.clone.refs_1_, ...), custom_call_target="tpu_custom_call" | custom-call | tf_op jit(solution)/shard_map/vcycle/pallas_call | solution.py:612
  141.2 1.9 %copy.19 = f32[24,24,256]{2,1,0:T(8,128)} copy(f32[24,24,256]{2,1,0:T(8,128)} %vcycle.1) | data formatting | bytes 1179648
  (2 shorter events, 0.0 us)
Async XLA Ops:
  0.0 0.8 copy-start

commit v2 on v1

v2 whole, which is shorter than its diff:
```python
import functools

import jax
import jax.numpy as jnp
import numpy as np
from jax import lax
from jax.experimental import pallas as pl
from jax.experimental.pallas import tpu as pltpu
from jax.sharding import PartitionSpec as P

TILE = 128
SWEEPS = 3
LEVELS = 4
SUBDIV = (0.125, 0.5, 0.75, 0.5, 0.125)
OMEGA = 0.5
MESH = pl.DeviceIdType.MESH
AROUND = ((0, 1), (0, -1), (1, 0), (-1, 0), (1, 1), (1, -1), (-1, 1), (-1, -1))
BASIS = (2496, 1176, 96)
KAPPA = OMEGA * 42 / 5040.0**3
FAR = 4


def up8(n):
    return -(-n // 8) * 8


def band(n, size, coeffs):
    i, j = np.indices((size, size))
    out = np.zeros((size, size), np.float32)
    for k, c in enumerate(coeffs):
        out[(j - i + 3 == k) & (i < n) & (j < n)] = c
    return out


def subdivision(n, rows, columns):
    i, j = np.indices((rows, columns))
    out = np.zeros((rows, columns), np.float32)
    for k, c in enumerate(SUBDIV):
        out[(i - 2 * j + 2 == k) & (i < 2 * n) & (j < n)] = c
    return out


def coarse_weights(width):
    wide, narrow = width >> 2, width >> 3
    tables = []
    for n in (wide, narrow):
        copies = np.eye(128 // n, dtype=np.float32)
        five = band(n, n, (0, 96, 1176, 2496, 1176, 96, 0))
        stiff = band(n, n, (-1, -24, -15, 80, -15, -24, -1))
        tables.append(np.stack([np.kron(copies, five), np.kron(copies, stiff)]))
    move = subdivision(narrow, wide, narrow)
    halves = np.eye(128 // wide, dtype=np.float32)
    down = np.kron(halves, np.concatenate([move, move], axis=1))
    zero = np.zeros_like(move.T)
    even = np.kron(halves, np.concatenate([move.T, zero], axis=0))
    odd = np.kron(halves, np.concatenate([zero, move.T], axis=0))
    tables.append(np.stack([down, even, odd]))
    return [t.astype(jnp.bfloat16) for t in tables]


def parts(x):
    high = x.astype(jnp.bfloat16)
    return high, (x - high.astype(jnp.float32)).astype(jnp.bfloat16)


def mul(a, b):
    return jnp.dot(a, b, preferred_element_type=jnp.float32)


def sums(x):
    return x[3], x[2] + x[4], x[1] + x[5], x[0] + x[6]


def five_taps(s):
    return BASIS[0] * s[0] + BASIS[1] * s[1] + BASIS[2] * s[2]


def stiff_taps(s):
    return 80.0 * s[0] - 15.0 * s[1] - 24.0 * s[2] - s[3]


def first_pass(x):
    s = sums(x)
    d, e = 2 * KAPPA * s[3], 3 * KAPPA * s[3]
    for k, (p, q) in enumerate(((2336, 4752), (1206, 2397), (144, 264))):
        d, e = d + p * KAPPA * s[k], e + q * KAPPA * s[k]
    return d, e


def second_pass(d, e):
    d, e = sums(d), sums(e)
    g = five_taps(e) - (4912.0 * d[0] + 2367.0 * d[1] + 216.0 * d[2] + d[3])
    q = five_taps(d) - stiff_taps(e)
    return g, q


def split_mul(x, table):
    high, low = parts(x)
    n = x.shape[0]
    both = mul(jnp.concatenate([high, low], axis=0), table)
    return both[:n] + both[n:]


def last_pass(g, q, table):
    return split_mul(g, table[0]) + split_mul(q, table[1])


def rows_at_once(count, rows):
    best = 1
    for n in range(1, count + 1):
        if count % n == 0 and n * rows <= 240:
            best = n
    return best


def loop(count, body, unroll=1):
    while count % unroll:
        unroll -= 1
    lax.fori_loop(0, count, lambda i, _: (body(i), 0)[1], 0, unroll=unroll)


def apply_packed(x, d, e, table, at, base, rows, count, use):
    def one(u):
        d[u + 3], e[u + 3] = first_pass([x[at + u, base - 3 + k : base - 3 + k + rows, :] for k in range(7)])

    loop(count, one, 3)
    size = rows_at_once(count, rows)

    def some(i):
        u = i * size
        gs, qs = [], []
        for j in range(size):
            g, q = second_pass([d[u + j + k] for k in range(7)], [e[u + j + k] for k in range(7)])
            gs.append(g)
            qs.append(q)
        value = last_pass(jnp.concatenate(gs, axis=0), jnp.concatenate(qs, axis=0), table)
        for j in range(size):
            use(u + j, value[j * rows : (j + 1) * rows])

    loop(count // size, some)


def coarse_cycle(shape, load2, tables, refs, midway):
    nu, nh = shape
    cu, nq = nu // 2, nh // 4
    nqp = up8(nq)
    x2, d2, e2, b2, t2, x3, f3, d3, e3, z3 = refs
    edge = (x2.shape[0] - nu) // 2

    def put2(u, new):
        x2[edge + u, 8 : 8 + nh] = new
        x2[edge + u, 0:8] = pltpu.roll(new[nh - 8 : nh], 64, 1)
        x2[edge + u, 8 + nh : 16 + nh] = pltpu.roll(new[0:8], 64, 1)

    def put3(u, new):
        x3[u, 8 : 8 + nqp] = new
        left, right = pltpu.roll(new, 32, 1), pltpu.roll(new[0:8], 96, 1)
        x3[u, 5:8] = left[nq - 3 : nq]
        x3[u, 8 + nq : 11 + nq] = right[0:3]

    def smooth2():
        def use(u, value):
            put2(u, x2[edge + u, 8 : 8 + nh] + ((OMEGA / 4) * load2[u] - value))
        apply_packed(x2, d2, e2, tables[0], edge, 8, nh, nu, use)

    loop(nu, lambda u: put2(u, (OMEGA / 4) * load2[u]), 4)
    loop(SWEEPS - 1, lambda i: smooth2())

    size = rows_at_once(nu, nh)

    def keep(u, value):
        t2[u] = load2[u] - 8.0 * value

    apply_packed(x2, d2, e2, tables[0], edge, 8, nh, nu, keep)

    def narrow(i):
        at = pl.ds(i * size, size)
        n = split_mul(t2[at].reshape(size * nh, 128), tables[2][0]).reshape(size, nh, 128)
        b2[pl.ds(i * size + 2, size), 8 : 8 + nh] = n
        for j in range(size):
            b2[i * size + 2 + j, 0:8] = pltpu.roll(n[j, nh - 8 : nh], 64, 1)
            b2[i * size + 2 + j, 8 + nh : 16 + nh] = pltpu.roll(n[j, 0:8], 64, 1)

    loop(nu // size, narrow)
    midway()
    lane = lax.broadcasted_iota(jnp.int32, (nq, 128), 1)
    first = lax.rem(lane // 32, 2) == 0

    def restrict(i):
        total = None
        for k in range(5):
            term = SUBDIV[k] * b2[2 * i + k]
            total = term if total is None else total + term
        z3[i] = total
        lines = []
        for start in (6, 6 + 2 * nq):
            line = None
            for m in range(5):
                term = SUBDIV[m] * z3[i, pl.ds(start + m, nq, stride=2), :]
                line = term if line is None else line + term
            lines.append(line)
        f3[i, 0:nq] = jnp.where(first, lines[0], lines[1])

    loop(cu, restrict, 4)
    loop(cu, lambda u: put3(u, (OMEGA / 8) * f3[u]), 4)

    def smooth3(i):
        def use(u, value):
            put3(u, x3[u, 8 : 8 + nqp] + ((OMEGA / 8) * f3[u] - value))
        apply_packed(x3, d3, e3, tables[1], 0, 8, nqp, cu, use)

    loop(2 * SWEEPS - 1, smooth3)

    nf = 2 * nq
    for u in range(cu):
        b, h, a = (x3[u, 7 + s : 7 + s + nq] for s in range(3))
        b2[2 + u, pl.ds(0, nq, stride=2), :] = 0.125 * (b + a) + 0.75 * h
        b2[2 + u, pl.ds(1, nq, stride=2), :] = 0.5 * (h + a)
    fine = up8(nf)
    for u in range(cu):
        here = b2[2 + u, 0:fine]
        after = b2[3 + u, 0:fine] if u + 1 < cu else jnp.zeros_like(here)
        before = b2[1 + u, 0:fine] if u > 0 else jnp.zeros_like(here)
        t2[2 * u, 0:fine] = 0.125 * (before + after) + 0.75 * here
        t2[2 * u + 1, 0:fine] = 0.5 * (here + after)

    def widen(i):
        at = pl.ds(i * size, size)
        z = t2[at, 0:fine].reshape(size * fine, 128)
        y = (split_mul(z, tables[2][1]).reshape(size, fine, 128), split_mul(z, tables[2][2]).reshape(size, fine, 128))
        for j in range(size):
            u = edge + i * size + j
            for s in range(2):
                x2[u, 8 + s * nf : 8 + (s + 1) * nf] += y[s][j, 0:nf]
            put2(i * size + j, x2[u, 8 : 8 + nh])

    loop(nu // size, widen)
    loop(SWEEPS, lambda i: smooth2())


def fine_weights(width):
    tables = []
    for n in (width, width // 2):
        five = band(n, n, (0, 96, 1176, 2496, 1176, 96, 0))
        stiff = band(n, n, (-1, -24, -15, 80, -15, -24, -1))
        move = subdivision(n // 2, n, max(n // 2, 128))
        tables += [np.stack([five, stiff]), move, np.ascontiguousarray(move.T)]
    return [t.astype(jnp.bfloat16) for t in tables]


def spots(n, at, rows, gap, reach):
    out = np.zeros((rows, 128), np.float32)
    for p in range(at - reach, at + n + reach):
        b, v = divmod(p - at, n)
        out[p, gap * (b % (128 // gap)) + v] = 1
    return out


class Halo:
    def __init__(self, refs, near):
        self.near, self.reach = near, near + FAR
        (self.send_near, self.send_far, self.near_v, self.far_v, self.near_u, self.far_u) = refs

    @staticmethod
    def scratch(planes, nu, nv, near):
        rows = nu + 2 * (near + FAR)
        shapes = [(2, planes, nu, near, 128), (2, planes, nu, FAR, 128), (2, planes, rows, near, 128)]
        shapes += [(2, planes, rows, FAR, 128), (2, planes, near, nv, 128), (2, planes, FAR, nv, 128)]
        return [pltpu.VMEM(shape, jnp.float32) for shape in shapes]


def kernel(dims, rs, guess, mask0, mask1, *refs):
    n_dir, n_patch, nu, nv, planes = dims
    mu, mv = nu // 2, nv // 2
    cu, cv = mu // 2, mv // 2
    band0, down0, up0, band1, down1, up1 = refs[:6]
    tables, (pick, pick0, pick1), out, refs = refs[6:9], refs[9:12], refs[12], refs[13:]
    x0, s0, f0, d0, e0, x1, s1, f1, d1, e1, r1, r2, t1, tv, tw = refs[:15]
    refs = refs[15:]
    side_send, side_recv, up_recv = refs[:3]
    xh, fh = Halo(refs[3:9], 5), Halo(refs[9:15], 2)
    lines0, lines1, line0, line1 = refs[15:19]
    slab_f, slab_x, strip_x, slab_far = refs[19:23]
    c2, packed, slots, load2 = refs[23:27]
    coarse = refs[27:37]
    send_sem, recv_sem, all_send, all_recv = refs[37:]

    U0, V0, U1, V1 = 9, 16, mu + 3, mv + 10
    wide = (V0 - 8, nv + 16)
    me_u, me_v = lax.axis_index("dir"), lax.axis_index("patch")
    n_all = n_dir * n_patch
    me = me_u * n_patch + me_v

    def place(flat):
        return lax.div(flat, n_patch), lax.rem(flat, n_patch)

    def present(a):
        return None if a == 0 else (me_u < n_dir - a if a > 0 else me_u >= -a)

    def given(flag, body):
        body() if flag is None else pl.when(flag)(body)

    taken = [0]

    def number(count):
        taken[0] += count
        return taken[0] - count

    def copies(items, first):
        made = []
        for k, (src, dst, a, b) in enumerate(items):
            made.append((a, functools.partial(
                pltpu.make_async_remote_copy,
                src_ref=src, dst_ref=dst, send_sem=send_sem.at[first + k], recv_sem=recv_sem.at[first + k],
                device_id={"dir": me_u + a, "patch": lax.rem(me_v + b + 2 * n_patch, n_patch)},
                device_id_type=MESH)))
        return made

    def grouped(made, sign, act):
        for step in sorted({a for a, _ in made}, key=abs):
            def body():
                for a, make in made:
                    if a == step:
                        act(make())
            given(present(sign * step), body)

    def start(made):
        grouped(made, 1, lambda c: c.start())

    def sent(made):
        grouped(made, 1, lambda c: c.wait_send())

    def received(made):
        grouped(made, -1, lambda c: c.wait_recv())

    barrier = pltpu.get_barrier_semaphore()

    def greet(i):
        u, v = place(lax.rem(me + 1 + i, n_all))
        pl.semaphore_signal(barrier, inc=1, device_id={"dir": u, "patch": v}, device_id_type=MESH)

    loop(n_all - 1, greet)

    for k, at in enumerate((0, 32, 96)):
        line0[k] = jnp.zeros(line0.shape[1:], jnp.float32)
        line0[k, :, :, at : at + nv] = mask0[...].astype(jnp.float32)
    for k, at in enumerate((0, 16, 32, 96, 112)):
        line1[k] = jnp.zeros(line1.shape[1:], jnp.float32)
        line1[k, :, :, at : at + mv] = mask1[...].astype(jnp.float32)
    ones = jnp.ones((128, 128), jnp.bfloat16)

    def spread(pattern, line):
        return (pattern * line).astype(jnp.bfloat16)

    def own(i):
        marks = [[spread(pick[...], line0[0, i * 4 + j, w : w + 1, :]) for j in range(4)] for w in range(planes)]
        full = mul(jnp.concatenate([m for row in marks for m in row], axis=0), ones)
        for w in range(planes):
            for j in range(4):
                u, k = i * 4 + j, w * 4 + j
                m = full[k * nv : (k + 1) * nv]
                lanes = slice(w * 128, w * 128 + 128)
                x0[w, U0 + u, V0 : V0 + nv] = m * guess[u, :, lanes]
                f0[w, U0 + u, V0 : V0 + nv] = OMEGA * m * rs[u, :, lanes]
                s0[w, U0 + u, V0 : V0 + nv] = m

    for ref in (x0, s0, f0, x1, s1, f1):
        def clear(u):
            ref[:, u] = jnp.zeros((ref.shape[0],) + ref.shape[2:], jnp.float32)
        loop(ref.shape[1], clear, 3)
    loop(nu // 4, own)
    for ref in (coarse[0], coarse[1], coarse[2], coarse[3], coarse[6], coarse[7], coarse[8], c2, tv):
        ref[...] = jnp.zeros_like(ref)
    pl.semaphore_wait(barrier, n_all - 1)

    def mask_items():
        first, second = [], []
        for b in (0, 1, -1):
            for a in (0, 1, -1):
                if a or b:
                    rows = slice(0, nu) if a == 0 else (slice(nu - U0, nu) if a > 0 else slice(0, U0))
                    to = slice(U0, U0 + nu) if a == 0 else (slice(0, U0) if a > 0 else slice(U0 + nu, U0 + nu + U0))
                    first.append((line0.at[{0: 0, 1: 2, -1: 1}[b], rows], lines0.at[(-b) % 3, to], a, b))
        for b in range(-2, 3):
            for a in range(-2, 3):
                if a or b:
                    rows, to = block_rows(a)
                    second.append((line1.at[(-b) % 5, rows], lines1.at[(-b) % 5, to], a, b))
        return first + second

    def block_rows(a):
        edge = U1 - mu
        if abs(a) < 2:
            return slice(0, mu), slice(U1 - a * mu, U1 - a * mu + mu)
        return (slice(mu - edge, mu), slice(0, edge)) if a > 0 else (slice(0, edge), slice(U1 + 2 * mu, U1 + 2 * mu + edge))

    masks = copies(mask_items(), number(8 + 24))

    def expand():
        received(masks)
        for a, at, n in ((0, U0, nu), (-1, 0, U0), (1, U0 + nu, U0)):
            def body():
                def one(i):
                    u = at + 3 * i
                    marks = []
                    for w in range(planes):
                        for j in range(3):
                            line = lines0[1, u + j, w : w + 1, :] + lines0[2, u + j, w : w + 1, :]
                            if a == 0:
                                line = line + line0[0, u + j - U0, w : w + 1, :]
                            else:
                                line = line + lines0[0, u + j, w : w + 1, :]
                            marks.append(spread(pick0[...], line))
                    full = mul(jnp.concatenate(marks, axis=0), ones)
                    n0 = s0.shape[2]
                    for w in range(planes):
                        for j in range(3):
                            s0[w, u + j] = full[(w * 3 + j) * n0 : (w * 3 + j + 1) * n0]
                loop(n // 3, one)
            given(present(a), body)
        for a in (0, -1, 1, -2, 2):
            rows, to = block_rows(-a)
            def body():
                def one(i):
                    marks = []
                    for j in range(3):
                        u = to.start + 3 * i + j
                        line = line1[0, u - U1] if a == 0 else lines1[0, u]
                        for b in range(1, 5):
                            line = line + lines1[b, u]
                        marks.append(spread(pick1[...], line))
                    full = mul(jnp.concatenate(marks, axis=0), ones)
                    n1 = s1.shape[2]
                    for j in range(3):
                        s1[0, to.start + 3 * i + j] = full[j * n1 : (j + 1) * n1]
                loop((to.stop - to.start) // 3, one)
            given(present(a), body)

    def operate(x, d, e, table, u0, count, window, use):
        lo, size = window
        n = x.shape[0]

        def one(i):
            u = u0 - 3 + i
            for w in range(n):
                t = [x[w, u, lo - 3 + k : lo - 3 + k + size, :] for k in range(7)]
                d[w, u, 0:size], e[w, u, 0:size] = first_pass(t)

        loop(count + 6, one, 3)
        rows = rows_at_once(count, size)

        def some(i):
            u = u0 + i * rows
            gs, qs = [], []
            for w in range(n):
                both = [second_pass([d[w, u + j + k, 0:size] for k in range(-3, 4)], [e[w, u + j + k, 0:size] for k in range(-3, 4)])
                        for j in range(rows)]
                gs.append(jnp.concatenate([g for g, _ in both], axis=0))
                qs.append(jnp.concatenate([q for _, q in both], axis=0))
            use(u, rows, last_pass(jnp.concatenate(gs, axis=1), jnp.concatenate(qs, axis=1), table))

        loop(count // rows, some)

    def sweep(x, s, f, d, e, table, u0, count, window, result=None):
        lo, size = window

        def use(u, rows, value):
            for j in range(rows):
                for w in range(x.shape[0]):
                    v = value[j * size : (j + 1) * size, w * 128 : (w + 1) * 128]
                    at = (w, u + j, slice(lo, lo + size))
                    new = x[at] + (f[at] - s[at] * v)
                    if result is None:
                        x[at] = new
                    else:
                        result[u + j - u0, :, w * 128 : (w + 1) * 128] = new

        operate(x, d, e, table, u0, count, window, use)

    def residual(x, s, f, d, e, table, down, scale, u0, count, window, narrow):
        lo, size = window

        def use(u, rows, value):
            lines = []
            for j in range(rows):
                line = []
                for w in range(x.shape[0]):
                    v = value[j * size : (j + 1) * size, w * 128 : (w + 1) * 128]
                    at = (w, u + j, slice(lo, lo + size))
                    line.append(scale * (f[at] - s[at] * v))
                lines.append(jnp.concatenate(line, axis=1))
            n = split_mul(jnp.concatenate(lines, axis=0), down[...])
            for j in range(rows):
                narrow[u + j - u0, 0:size] = n[j * size : (j + 1) * size]

        operate(x, d, e, table, u0, count, window, use)

    def restrict(narrow, i, size, first, n):
        total = None
        for k in range(5):
            term = SUBDIV[k] * narrow[2 * i + k, 0:size]
            total = term if total is None else total + term
        t1[i, 0:size] = total
        line = None
        for m in range(5):
            term = SUBDIV[m] * t1[i, pl.ds(first + m, n, stride=2), :]
            line = term if line is None else line + term
        return line

    def near_items(x, h, strips, sides, ups):
        items = []
        top = U0 + nu
        for a, b in AROUND:
            k = 0 if b > 0 else 1
            if b == 0:
                rows = slice(top - h, top) if a > 0 else slice(U0, U0 + h)
                items.append((x.at[:, rows, V0 : V0 + nv], ups.at[0 if a > 0 else 1], a, b))
                continue
            reach = (sides.shape[-3] - nu) // 2
            rows = slice(0, nu) if a == 0 else (slice(nu - h, nu) if a > 0 else slice(0, h))
            at = reach if a == 0 else (reach - h if a > 0 else reach + nu)
            to = slice(at, at + rows.stop - rows.start)
            items.append((strips.at[1 - k, :, rows], sides.at[k, :, to], a, b))
        return items

    def stage(x, h, strips, skip=0):
        def one(u):
            for w in range(planes):
                strips[0, w, u] = x[w, U0 + u, V0 + skip : V0 + skip + h]
                strips[1, w, u] = x[w, U0 + u, V0 + nv - skip - h : V0 + nv - skip]
        loop(nu, one, 4)

    def lay_sides(x, h, sides, reach, skip=0, extra=None):
        extra = reach if extra is None else extra
        for a, at, n in ((0, U0, nu), (-1, U0 - extra, extra), (1, U0 + nu, extra)):
            def body():
                def one(i):
                    u = at + i
                    for w in range(planes):
                        x[w, u, V0 - skip - h : V0 - skip] = sides[0, w, u - U0 + reach]
                        x[w, u, V0 + nv + skip : V0 + nv + skip + h] = sides[1, w, u - U0 + reach]
                loop(n, one, 4)
            given(present(a), body)

    def lay_ups(x, h, ups, skip=0):
        def low():
            x[:, U0 - skip - h : U0 - skip, V0 : V0 + nv] = ups[0]
        def high():
            x[:, U0 + nu + skip : U0 + nu + skip + h, V0 : V0 + nv] = ups[1]
        given(present(-1), low)
        given(present(1), high)

    base = number(8 * SWEEPS)
    f_near = copies(near_items(f0, fh.near, fh.send_near, fh.near_v, fh.near_u), number(8))
    block0 = (V0, nv)

    def smooth0(i):
        stage(x0, 3, side_send.at[i])
        made = copies(near_items(x0, 3, side_send.at[i], side_recv.at[i], up_recv.at[i]), base + 8 * i)
        start(made)

        @pl.when(i == 0)
        def _():
            start(masks)
            stage(f0, fh.near, fh.send_near)
            start(f_near)

        pl.when(i == 1)(expand)
        received(made)
        sent(made)
        lay_sides(x0, 3, side_recv.at[i], 3)
        lay_ups(x0, 3, up_recv.at[i])
        sweep(x0, s0, f0, d0, e0, band0, U0, nu, block0)

    loop(SWEEPS, smooth0)

    stage(x0, xh.near, xh.send_near)
    x_near = copies(near_items(x0, xh.near, xh.send_near, xh.near_v, xh.near_u), number(8))
    start(x_near)
    stage(x0, FAR, xh.send_far, xh.near)
    stage(f0, FAR, fh.send_far, fh.near)
    received(f_near)
    lay_sides(f0, fh.near, fh.near_v, fh.reach, 0, fh.near)
    lay_ups(f0, fh.near, fh.near_u)
    received(x_near)
    lay_sides(x0, xh.near, xh.near_v, xh.reach, 0, xh.near)
    lay_ups(x0, xh.near, xh.near_u)
    residual(x0, s0, f0, d0, e0, band0, down0, 2.0, U0 - 2, nu + 4, wide, r1)

    mid = slice(U1, U1 + mu)

    def load1(i):
        line = (OMEGA / 2) * s1[0, U1 + i, V1 : V1 + mv] * restrict(r1, i, wide[1], V0 - wide[0] - 2, mv)
        slab_f[0, U1 + i] = line

    loop(mu, load1, 4)

    def slab_items(slab, b_from, steps):
        items = []
        for a in steps:
            rows, to = block_rows(a)
            items.append((slab.at[b_from, slice(U1 + rows.start, U1 + rows.stop)], slab.at[b_from, to], a, 0))
        return items

    f_v = copies([(slab_f.at[0, mid], slab_f.at[(-b) % 3, mid], 0, b) for b in (1, -1)]
                 + slab_items(slab_f, 0, (1, -1)), number(4))
    f_u = copies(slab_items(slab_f, 1, (1, -1)) + slab_items(slab_f, 2, (1, -1)), number(4))
    start(f_v)
    received(f_v[:2])
    start(f_u)
    received(f_v[2:])
    received(f_u)

    def lay_slab(slab, targets, steps):
        for a in steps:
            rows, to = block_rows(-a)
            def body():
                def one(i):
                    u = to.start + i
                    for x in targets:
                        for b in (-1, 0, 1):
                            x[0, u, V1 + b * mv : V1 + (b + 1) * mv] = slab[b % 3, u]
                loop(to.stop - to.start, one, 3)
            given(present(a), body)

    lay_slab(slab_f, (f1, x1), (0, -1, 1))

    def window1(h):
        lo = (V1 - h) // 8 * 8
        return lo, up8(V1 + mv + h) - lo

    level1 = (x1, s1, f1, d1, e1, band1)
    sweep(*level1, U1 - 8, mu + 16, window1(8))
    sweep(*level1, U1 - 6, mu + 12, window1(5))

    def own_x1(u):
        slab_x[0, U1 + u] = x1[0, U1 + u, V1 : V1 + mv]
        strip_x[0, u] = x1[0, U1 + u, V1 : V1 + 3]
        strip_x[1, u] = x1[0, U1 + u, V1 + mv - 3 : V1 + mv]

    loop(mu, own_x1, 3)
    at1 = window1(2)
    residual(*level1, down1, 4.0, U1 - 2, mu + 4, at1, r2)

    def load_2(i):
        c2[i, 0:cv] = restrict(r2, i, at1[1], V1 - at1[0] - 2, cv)

    loop(cu, load_2, 3)

    half = cu // 2
    for j in range(half):
        packed[j] = (c2[j] + pltpu.roll(c2[j + half], 64, 1))[0:cv]
        slots[me_u, 1, j] = packed[j]

    def gather(i, incoming):
        flat = lax.rem(me + 1 + i, n_all) if not incoming else lax.rem(me + n_all - 1 - i, n_all)
        u, v = place(flat)
        source_u, source_v, target_v = (u, v, me_v) if incoming else (me_u, me_v, v)
        return pltpu.make_async_remote_copy(
            src_ref=packed,
            dst_ref=slots.at[source_u, lax.rem(source_v - target_v + 1 + n_patch, n_patch)],
            send_sem=all_send.at[i],
            recv_sem=all_recv.at[i],
            device_id={"dir": u, "patch": v},
            device_id_type=MESH,
        )

    loop(n_all - 1, lambda i: gather(i, False).start())
    loop(n_all - 1, lambda i: gather(i, False).wait_send())
    loop(n_all - 1, lambda i: gather(i, True).wait_recv())

    x_v = copies([(slab_x.at[0, mid], slab_x.at[(-b) % 3, mid], 0, b) for b in (1, -1)]
                 + [(strip_x.at[1], slab_far.at[0, mid], 0, 2), (strip_x.at[0], slab_far.at[1, mid], 0, -2)], number(4))
    x_u = []
    for b in range(3):
        x_u += slab_items(slab_x, b, (1, -1, 2, -2))
    for b in range(2):
        x_u += slab_items(slab_far, b, (1, -1, 2, -2))
    x_u = copies(x_u, number(len(x_u)))

    def far_items(x, halo):
        h, near = halo.reach, halo.near
        body = slice(h, h + nu)
        first = [(halo.send_far.at[1], halo.far_v.at[0, :, body], 0, 1), (halo.send_far.at[0], halo.far_v.at[1, :, body], 0, -1)]
        top = U0 + nu
        first.append((x.at[:, top - h : top - near, V0 : V0 + nv], halo.far_u.at[0], 1, 0))
        first.append((x.at[:, U0 + near : U0 + h, V0 : V0 + nv], halo.far_u.at[1], -1, 0))
        second = []
        for k in range(2):
            second.append((halo.far_v.at[k, :, nu : nu + h], halo.far_v.at[k, :, 0:h], 1, 0))
            second.append((halo.far_v.at[k, :, h : 2 * h], halo.far_v.at[k, :, h + nu : nu + 2 * h], -1, 0))
            second.append((halo.near_v.at[k, :, nu : nu + FAR], halo.near_v.at[k, :, 0:FAR], 1, 0))
            second.append((halo.near_v.at[k, :, h + near : 2 * h], halo.near_v.at[k, :, h + nu + near : nu + 2 * h], -1, 0))
        return first, second

    xf, xs = far_items(x0, xh)
    ff, fs = far_items(f0, fh)
    far_first = copies(xf + ff, number(8))
    far_second = copies(xs + fs, number(16))
    start(x_v)
    start(far_first)

    low = lax.broadcasted_iota(jnp.int32, (cv, 128), 1) < 64
    for d in range(n_dir):
        for k in range(n_patch // 2):
            for j in range(half):
                a, b = slots[d, k, j], slots[d, k + n_patch // 2, j]
                load2[d * cu + j, k * cv : (k + 1) * cv] = jnp.where(low, a, pltpu.roll(b, 64, 1))
                load2[d * cu + half + j, k * cv : (k + 1) * cv] = jnp.where(low, pltpu.roll(a, 64, 1), b)

    def second_leg():
        received(x_v)
        start(x_u)
        received([far_first[0], far_first[1], far_first[4], far_first[5]])
        start(far_second)

    coarse_cycle((cu * n_dir, cv * n_patch // 2), load2, tables, coarse, second_leg)

    span = (tv.shape[1] - 12) // 2

    def prolong(line, first, table, x, s):
        def one(i):
            b, h, a = (line(i, first + k) for k in range(3))
            tv[i, pl.ds(6, span, stride=2), :] = 0.125 * (b + a) + 0.75 * h
            tv[i, pl.ds(7, span, stride=2), :] = 0.5 * (h + a)

        loop(24, one, 3)
        n = tv.shape[1]

        def widen(i):
            y = split_mul(tv[pl.ds(4 * i, 4)].reshape(4 * n, 128), table[...])
            for w in range(x.shape[0]):
                for j in range(4):
                    tw[w, 4 * i + j] = y[j * n : (j + 1) * n, w * 128 : (w + 1) * 128]

        loop(6, widen)

        def add(t):
            for w in range(x.shape[0]):
                p, q, r = tw[w, t], tw[w, t + 1], tw[w, t + 2]
                for j, y in enumerate((0.5 * (p + q), 0.125 * (p + r) + 0.75 * q)):
                    u = 2 * t + j
                    x[w, u] = x[w, u] + jnp.where(s[w, u] > 0.5, y, 0.0)

        loop(21, add)

    received(x_u)
    lay_slab(slab_x, (x1,), (0, -1, 1, -2, 2))
    for a in (0, -1, 1, -2, 2):
        rows, to = block_rows(-a)
        def body():
            def one(i):
                u = to.start + i
                x1[0, u, V1 - mv - 3 : V1 - mv] = slab_far[0, u]
                x1[0, u, V1 + 2 * mv : V1 + 2 * mv + 3] = slab_far[1, u]
            loop(to.stop - to.start, one, 3)
        given(present(a), body)
    x2 = coarse[0]
    edge = (x2.shape[0] - cu * n_dir) // 2
    prolong(lambda i, k: x2[edge + me_u * cu - (U1 + 1) // 2 + i, k : k + span], 5, up1, x1, s1)
    sweep(*level1, U1 - 12, mu + 24, window1(12))
    sweep(*level1, U1 - 9, mu + 18, window1(9))
    sweep(*level1, U1 - 6, mu + 12, window1(6))
    received([far_first[k] for k in (2, 3, 6, 7)])
    received(far_second)
    for x, halo in ((x0, xh), (f0, fh)):
        lay_sides(x, FAR, halo.far_v, halo.reach, halo.near)
        lay_sides(x, halo.near, halo.near_v, halo.reach)
        lay_ups(x, FAR, halo.far_u, halo.near)
    for made in (masks, f_near, x_near, f_v, f_u, x_v, x_u, far_first, far_second):
        sent(made)
    prolong(lambda i, k: x1[0, U1 - (U0 + 1) // 2 + i, k : k + span], 16, up0, x0, s0)
    level0 = (x0, s0, f0, d0, e0, band0)
    sweep(*level0, U0 - 6, nu + 12, wide)
    sweep(*level0, U0 - 3, nu + 6, wide)
    sweep(*level0, U0, nu, block0, out)
    assert taken[0] <= send_sem.shape[0]


def on_device(right_side, guess, mask_fine, mask_next):
    nu, nv, nw = right_side.shape
    n_dir, n_patch = lax.axis_size("dir"), lax.axis_size("patch")
    planes = nw // 128
    mu, mv = nu // 2, nv // 2
    cu, cv = mu // 2, mv // 2
    gu, gh = cu * n_dir, cv * n_patch // 2
    eu, eq = gu // 2, up8(gh // 4)
    rows0, cols0, rows1, cols1 = nu + 18, nv + 32, mu + 30, up8(mv + 37)
    operands = [right_side, guess, jnp.transpose(mask_fine, (0, 2, 1)), jnp.transpose(mask_next, (0, 2, 1))]
    operands += [jnp.asarray(t) for t in fine_weights(nw)]
    operands += [jnp.asarray(t) for t in coarse_weights(nw)]
    operands += [jnp.asarray(np.eye(nv, 128, dtype=np.float32))]
    operands += [jnp.asarray(spots(nv, 16, cols0, 32, 9)[:, :]), jnp.asarray(spots(mv, 22, cols1, 16, 15))]

    def vmem(*shape):
        return pltpu.VMEM(shape, jnp.float32)

    scratch = [vmem(planes, rows0, cols0, 128)] * 3 + [vmem(planes, rows0, nv + 16, 128)] * 2
    scratch += [vmem(1, rows1, cols1, 128)] * 3 + [vmem(1, rows1, cols1 - 16, 128)] * 2
    scratch += [vmem(nu + 4, nv + 16, 128), vmem(mu + 4, cols1 - 16, 128), vmem(mu, nv + 16, 128)]
    scratch += [vmem(24, cols1, 128), vmem(planes, 24, cols1, 128)]
    scratch += [vmem(SWEEPS, 2, planes, nu, 3, 128), vmem(SWEEPS, 2, planes, nu + 6, 3, 128)]
    scratch += [vmem(SWEEPS, 2, planes, 3, nv, 128)]
    scratch += Halo.scratch(planes, nu, nv, 5) + Halo.scratch(planes, nu, nv, 2)
    scratch += [vmem(3, rows0, planes, 128), vmem(5, rows1, 1, 128), vmem(3, nu, planes, 128), vmem(5, mu, 1, 128)]
    scratch += [vmem(3, rows1, mv, 128), vmem(3, rows1, mv, 128), vmem(2, mu, 3, 128), vmem(2, rows1, 3, 128)]
    scratch += [vmem(cu, up8(cv), 128), vmem(cu // 2, cv, 128), vmem(n_dir, n_patch, cu // 2, cv, 128)]
    scratch += [vmem(gu, gh, 128), vmem(gu + 20, gh + 16, 128), vmem(gu + 6, gh, 128), vmem(gu + 6, gh, 128)]
    scratch += [vmem(gu + 4, gh + 16, 128), vmem(gu, gh, 128), vmem(eu, eq + 16, 128), vmem(eu, eq, 128)]
    scratch += [vmem(eu + 6, eq, 128), vmem(eu + 6, eq, 128), vmem(eu, gh + 16, 128)]
    scratch += [pltpu.SemaphoreType.DMA((160,))] * 2 + [pltpu.SemaphoreType.DMA((n_dir * n_patch - 1,))] * 2
    space = pl.BlockSpec(memory_space=pltpu.VMEM)
    return pl.pallas_call(
        functools.partial(kernel, (n_dir, n_patch, nu, nv, planes)),
        out_shape=jax.ShapeDtypeStruct(right_side.shape, jnp.float32),
        in_specs=[space] * len(operands),
        out_specs=space,
        scratch_shapes=scratch,
        compiler_params=pltpu.CompilerParams(
            collective_id=0, has_side_effects=True, vmem_limit_bytes=60 * 2**20
        ),
        name="vcycle",
    )(*operands)


def solution(mesh):
    spec = P("dir", "patch", None)
    return jax.shard_map(
        on_device, mesh=mesh, in_specs=(spec,) * 4, out_specs=spec, check_vma=False
    )
```

time: 143 us -> 111 us (0.78)
  Pallas kernels: 137 us -> 109 us
  local copies, waits for them, and re-layouts: 4.96 us -> 1.92 us
    pallas_call x1, Pallas kernels: 137 us -> 109 us  [on_device(): pl.pallas_call(functools.partial(kernel, (n_dir, n_patch, nu, nv, planes)...]
where the time goes in v2:
time: 111 us
  Pallas kernels  109 us (98%)
  local copies, waits for them, and re-layouts  1.92 us (2%)
    pallas_call x1, Pallas kernels, on_device(): pl.pallas_call(functools.partial(kernel, (n_dir, n_patch, nu, nv, planes)...  109 us

profile of v2, /device:TPU:0, one launch (start us, length us, event | category | flops | bytes accessed | tf_op | source)
XLA Modules:
  0.0 110.9 jit_solution(16306502643737310073)
XLA Ops:
  0.0 109.0 %vcycle.1 = f32[24,24,256]{2,1,0:T(8,128)} custom-call(f32[24,24,256]{2,1,0:T(8,128)} %rs.1, f32[24,24,256]{2,1,0:T(8,128)} %guess.1, s32[24,2,24]{2,1,0:T(2,128)} %bitcast.2, s32[12,1,12]{2,1,0:T(1,128)} %bitcast.3, bf16[2,256,256]{2,1,0:T(8,128)(2,1)} %constant.24.clone.refs_0_, bf16[256,128]{1,0:T(8,128)(2,1)} %constant.25.clone.refs_1_, ...), custom_call_target="tpu_custom_call" | custom-call | tf_op jit(solution)/shard_map/vcycle/pallas_call | solution.py:813
  109.0 1.9 %copy.18 = f32[24,24,256]{2,1,0:T(8,128)} copy(f32[24,24,256]{2,1,0:T(8,128)} %vcycle.1) | data formatting | bytes 1179648

commit v3 on v2

--- a/solution.py
+++ b/solution.py
@@ -102,6 +102,9 @@
 
 
 def last_pass(g, q, table):
+    width = g.shape[1]
+    if width < 256:
+        return split_mul(jnp.concatenate([g, q], axis=1), table[...].reshape(2 * width, width))
     return split_mul(g, table[0]) + split_mul(q, table[1])
 
 
@@ -182,7 +185,6 @@
             b2[i * size + 2 + j, 8 + nh : 16 + nh] = pltpu.roll(n[j, 0:8], 64, 1)
 
     loop(nu // size, narrow)
-    midway()
     lane = lax.broadcasted_iota(jnp.int32, (nq, 128), 1)
     first = lax.rem(lane // 32, 2) == 0
 
@@ -211,6 +213,7 @@
 
     loop(2 * SWEEPS - 1, smooth3)
 
+    midway()
     nf = 2 * nq
     for u in range(cu):
         b, h, a = (x3[u, 7 + s : 7 + s + nq] for s in range(3))
@@ -269,12 +272,13 @@
         return [pltpu.VMEM(shape, jnp.float32) for shape in shapes]
 
 
-def kernel(dims, rs, guess, mask0, mask1, *refs):
+def kernel(dims, *refs):
     n_dir, n_patch, nu, nv, planes = dims
     mu, mv = nu // 2, nv // 2
     cu, cv = mu // 2, mv // 2
-    band0, down0, up0, band1, down1, up1 = refs[:6]
-    tables, (pick, pick0, pick1), out, refs = refs[6:9], refs[9:12], refs[12], refs[13:]
+    sources, out, held, refs = refs[:16], refs[16], refs[17:33], refs[33:]
+    rs, guess, mask0, mask1, pick, pick0, pick1, band0, down0, up0, band1, down1, up1 = held[:13]
+    tables = held[13:]
     x0, s0, f0, d0, e0, x1, s1, f1, d1, e1, r1, r2, t1, tv, tw = refs[:15]
     refs = refs[15:]
     side_send, side_recv, up_recv = refs[:3]
@@ -283,7 +287,7 @@
     slab_f, slab_x, strip_x, slab_far = refs[19:23]
     c2, packed, slots, load2 = refs[23:27]
     coarse = refs[27:37]
-    send_sem, recv_sem, all_send, all_recv = refs[37:]
+    send_sem, recv_sem, all_send, all_recv, load_sem = refs[37:]
 
     U0, V0, U1, V1 = 9, 16, mu + 3, mv + 10
     wide = (V0 - 8, nv + 16)
@@ -340,7 +344,20 @@
         pl.semaphore_signal(barrier, inc=1, device_id={"dir": u, "patch": v}, device_id_type=MESH)
 
     loop(n_all - 1, greet)
-
+    loads = [pltpu.make_async_copy(source, to, load_sem.at[k]) for k, (source, to) in enumerate(zip(sources, held))]
+    for k in (1, 2, 4, 0, 3, *range(5, 16)):
+        loads[k].start()
+
+
+    def clear(*refs):
+        for ref in refs:
+            def one(u):
+                ref[:, u] = jnp.zeros((ref.shape[0],) + ref.shape[2:], jnp.float32)
+            loop(ref.shape[1], one, 3)
+
+    clear(x0, s0, f0)
+    for k in range(5):
+        loads[k].wait()
     for k, at in enumerate((0, 32, 96)):
         line0[k] = jnp.zeros(line0.shape[1:], jnp.float32)
         line0[k, :, :, at : at + nv] = mask0[...].astype(jnp.float32)
@@ -364,13 +381,15 @@
                 f0[w, U0 + u, V0 : V0 + nv] = OMEGA * m * rs[u, :, lanes]
                 s0[w, U0 + u, V0 : V0 + nv] = m
 
-    for ref in (x0, s0, f0, x1, s1, f1):
-        def clear(u):
-            ref[:, u] = jnp.zeros((ref.shape[0],) + ref.shape[2:], jnp.float32)
-        loop(ref.shape[1], clear, 3)
     loop(nu // 4, own)
-    for ref in (coarse[0], coarse[1], coarse[2], coarse[3], coarse[6], coarse[7], coarse[8], c2, tv):
-        ref[...] = jnp.zeros_like(ref)
+
+    def prepare():
+        clear(x1, s1, f1)
+        for ref in (coarse[0], coarse[1], coarse[2], coarse[3], coarse[6], coarse[7], coarse[8], c2, tv):
+            ref[...] = jnp.zeros_like(ref)
+        for load in loads[5:]:
+            load.wait()
+
     pl.semaphore_wait(barrier, n_all - 1)
 
     def mask_items():
@@ -550,134 +569,6 @@
         given(present(-1), low)
         given(present(1), high)
 
-    base = number(8 * SWEEPS)
-    f_near = copies(near_items(f0, fh.near, fh.send_near, fh.near_v, fh.near_u), number(8))
-    block0 = (V0, nv)
-
-    def smooth0(i):
-        stage(x0, 3, side_send.at[i])
-        made = copies(near_items(x0, 3, side_send.at[i], side_recv.at[i], up_recv.at[i]), base + 8 * i)
-        start(made)
-
-        @pl.when(i == 0)
-        def _():
-            start(masks)
-            stage(f0, fh.near, fh.send_near)
-            start(f_near)
-
-        pl.when(i == 1)(expand)
-        received(made)
-        sent(made)
-        lay_sides(x0, 3, side_recv.at[i], 3)
-        lay_ups(x0, 3, up_recv.at[i])
-        sweep(x0, s0, f0, d0, e0, band0, U0, nu, block0)
-
-    loop(SWEEPS, smooth0)
-
-    stage(x0, xh.near, xh.send_near)
-    x_near = copies(near_items(x0, xh.near, xh.send_near, xh.near_v, xh.near_u), number(8))
-    start(x_near)
-    stage(x0, FAR, xh.send_far, xh.near)
-    stage(f0, FAR, fh.send_far, fh.near)
-    received(f_near)
-    lay_sides(f0, fh.near, fh.near_v, fh.reach, 0, fh.near)
-    lay_ups(f0, fh.near, fh.near_u)
-    received(x_near)
-    lay_sides(x0, xh.near, xh.near_v, xh.reach, 0, xh.near)
-    lay_ups(x0, xh.near, xh.near_u)
-    residual(x0, s0, f0, d0, e0, band0, down0, 2.0, U0 - 2, nu + 4, wide, r1)
-
-    mid = slice(U1, U1 + mu)
-
-    def load1(i):
-        line = (OMEGA / 2) * s1[0, U1 + i, V1 : V1 + mv] * restrict(r1, i, wide[1], V0 - wide[0] - 2, mv)
-        slab_f[0, U1 + i] = line
-
-    loop(mu, load1, 4)
-
-    def slab_items(slab, b_from, steps):
-        items = []
-        for a in steps:
-            rows, to = block_rows(a)
-            items.append((slab.at[b_from, slice(U1 + rows.start, U1 + rows.stop)], slab.at[b_from, to], a, 0))
-        return items
-
-    f_v = copies([(slab_f.at[0, mid], slab_f.at[(-b) % 3, mid], 0, b) for b in (1, -1)]
-                 + slab_items(slab_f, 0, (1, -1)), number(4))
-    f_u = copies(slab_items(slab_f, 1, (1, -1)) + slab_items(slab_f, 2, (1, -1)), number(4))
-    start(f_v)
-    received(f_v[:2])
-    start(f_u)
-    received(f_v[2:])
-    received(f_u)
-
-    def lay_slab(slab, targets, steps):
-        for a in steps:
-            rows, to = block_rows(-a)
-            def body():
-                def one(i):
-                    u = to.start + i
-                    for x in targets:
-                        for b in (-1, 0, 1):
-                            x[0, u, V1 + b * mv : V1 + (b + 1) * mv] = slab[b % 3, u]
-                loop(to.stop - to.start, one, 3)
-            given(present(a), body)
-
-    lay_slab(slab_f, (f1, x1), (0, -1, 1))
-
-    def window1(h):
-        lo = (V1 - h) // 8 * 8
-        return lo, up8(V1 + mv + h) - lo
-
-    level1 = (x1, s1, f1, d1, e1, band1)
-    sweep(*level1, U1 - 8, mu + 16, window1(8))
-    sweep(*level1, U1 - 6, mu + 12, window1(5))
-
-    def own_x1(u):
-        slab_x[0, U1 + u] = x1[0, U1 + u, V1 : V1 + mv]
-        strip_x[0, u] = x1[0, U1 + u, V1 : V1 + 3]
-        strip_x[1, u] = x1[0, U1 + u, V1 + mv - 3 : V1 + mv]
-
-    loop(mu, own_x1, 3)
-    at1 = window1(2)
-    residual(*level1, down1, 4.0, U1 - 2, mu + 4, at1, r2)
-
-    def load_2(i):
-        c2[i, 0:cv] = restrict(r2, i, at1[1], V1 - at1[0] - 2, cv)
-
-    loop(cu, load_2, 3)
-
-    half = cu // 2
-    for j in range(half):
-        packed[j] = (c2[j] + pltpu.roll(c2[j + half], 64, 1))[0:cv]
-        slots[me_u, 1, j] = packed[j]
-
-    def gather(i, incoming):
-        flat = lax.rem(me + 1 + i, n_all) if not incoming else lax.rem(me + n_all - 1 - i, n_all)
-        u, v = place(flat)
-        source_u, source_v, target_v = (u, v, me_v) if incoming else (me_u, me_v, v)
-        return pltpu.make_async_remote_copy(
-            src_ref=packed,
-            dst_ref=slots.at[source_u, lax.rem(source_v - target_v + 1 + n_patch, n_patch)],
-            send_sem=all_send.at[i],
-            recv_sem=all_recv.at[i],
-            device_id={"dir": u, "patch": v},
-            device_id_type=MESH,
-        )
-
-    loop(n_all - 1, lambda i: gather(i, False).start())
-    loop(n_all - 1, lambda i: gather(i, False).wait_send())
-    loop(n_all - 1, lambda i: gather(i, True).wait_recv())
-
-    x_v = copies([(slab_x.at[0, mid], slab_x.at[(-b) % 3, mid], 0, b) for b in (1, -1)]
-                 + [(strip_x.at[1], slab_far.at[0, mid], 0, 2), (strip_x.at[0], slab_far.at[1, mid], 0, -2)], number(4))
-    x_u = []
-    for b in range(3):
-        x_u += slab_items(slab_x, b, (1, -1, 2, -2))
-    for b in range(2):
-        x_u += slab_items(slab_far, b, (1, -1, 2, -2))
-    x_u = copies(x_u, number(len(x_u)))
-
     def far_items(x, halo):
         h, near = halo.reach, halo.near
         body = slice(h, h + nu)
@@ -695,10 +586,140 @@
 
     xf, xs = far_items(x0, xh)
     ff, fs = far_items(f0, fh)
-    far_first = copies(xf + ff, number(8))
+    x_far, f_far = copies(xf, number(4)), copies(ff, number(4))
     far_second = copies(xs + fs, number(16))
+    base = number(8 * SWEEPS)
+    f_near = copies(near_items(f0, fh.near, fh.send_near, fh.near_v, fh.near_u), number(8))
+    block0 = (V0, nv)
+
+    def smooth0(i):
+        stage(x0, 3, side_send.at[i])
+        made = copies(near_items(x0, 3, side_send.at[i], side_recv.at[i], up_recv.at[i]), base + 8 * i)
+        start(made)
+
+        @pl.when(i == 0)
+        def _():
+            start(masks)
+            stage(f0, fh.near, fh.send_near)
+            start(f_near)
+            prepare()
+
+        pl.when(i == 1)(expand)
+        received(made)
+        sent(made)
+        lay_sides(x0, 3, side_recv.at[i], 3)
+        lay_ups(x0, 3, up_recv.at[i])
+        sweep(x0, s0, f0, d0, e0, band0, U0, nu, block0)
+
+    loop(SWEEPS, smooth0)
+
+    stage(x0, xh.near, xh.send_near)
+    x_near = copies(near_items(x0, xh.near, xh.send_near, xh.near_v, xh.near_u), number(8))
+    start(x_near)
+    stage(x0, FAR, xh.send_far, xh.near)
+    stage(f0, FAR, fh.send_far, fh.near)
+    received(f_near)
+    lay_sides(f0, fh.near, fh.near_v, fh.reach, 0, fh.near)
+    lay_ups(f0, fh.near, fh.near_u)
+    received(x_near)
+    start(f_far)
+    lay_sides(x0, xh.near, xh.near_v, xh.reach, 0, xh.near)
+    lay_ups(x0, xh.near, xh.near_u)
+    residual(x0, s0, f0, d0, e0, band0, down0, 2.0, U0 - 2, nu + 4, wide, r1)
+
+    mid = slice(U1, U1 + mu)
+
+    def load1(i):
+        line = (OMEGA / 2) * s1[0, U1 + i, V1 : V1 + mv] * restrict(r1, i, wide[1], V0 - wide[0] - 2, mv)
+        slab_f[0, U1 + i] = line
+
+    loop(mu, load1, 4)
+
+    def slab_items(slab, b_from, steps):
+        items = []
+        for a in steps:
+            rows, to = block_rows(a)
+            items.append((slab.at[b_from, slice(U1 + rows.start, U1 + rows.stop)], slab.at[b_from, to], a, 0))
+        return items
+
+    f_v = copies([(slab_f.at[0, mid], slab_f.at[(-b) % 3, mid], 0, b) for b in (1, -1)]
+                 + slab_items(slab_f, 0, (1, -1)), number(4))
+    f_u = copies(slab_items(slab_f, 1, (1, -1)) + slab_items(slab_f, 2, (1, -1)), number(4))
+    start(f_v)
+    received(f_v[:2])
+    start(f_u)
+    received(f_v[2:])
+    received(f_u)
+    start(x_far)
+
+    def lay_slab(slab, targets, steps):
+        for a in steps:
+            rows, to = block_rows(-a)
+            def body():
+                def one(i):
+                    u = to.start + i
+                    for x in targets:
+                        for b in (-1, 0, 1):
+                            x[0, u, V1 + b * mv : V1 + (b + 1) * mv] = slab[b % 3, u]
+                loop(to.stop - to.start, one, 3)
+            given(present(a), body)
+
+    lay_slab(slab_f, (f1, x1), (0, -1, 1))
+
+    def window1(h):
+        lo = (V1 - h) // 8 * 8
+        return lo, up8(V1 + mv + h) - lo
+
+    level1 = (x1, s1, f1, d1, e1, band1)
+    sweep(*level1, U1 - 8, mu + 16, window1(8))
+    sweep(*level1, U1 - 6, mu + 12, window1(5))
+
+    def own_x1(u):
+        slab_x[0, U1 + u] = x1[0, U1 + u, V1 : V1 + mv]
+        strip_x[0, u] = x1[0, U1 + u, V1 : V1 + 3]
+        strip_x[1, u] = x1[0, U1 + u, V1 + mv - 3 : V1 + mv]
+
+    loop(mu, own_x1, 3)
+    at1 = window1(2)
+    residual(*level1, down1, 4.0, U1 - 2, mu + 4, at1, r2)
+
+    def load_2(i):
+        c2[i, 0:cv] = restrict(r2, i, at1[1], V1 - at1[0] - 2, cv)
+
+    loop(cu, load_2, 3)
+
+    half = cu // 2
+    for j in range(half):
+        packed[j] = (c2[j] + pltpu.roll(c2[j + half], 64, 1))[0:cv]
+        slots[me_u, 1, j] = packed[j]
+
+    def gather(i, incoming):
+        flat = lax.rem(me + 1 + i, n_all) if not incoming else lax.rem(me + n_all - 1 - i, n_all)
+        u, v = place(flat)
+        source_u, source_v, target_v = (u, v, me_v) if incoming else (me_u, me_v, v)
+        return pltpu.make_async_remote_copy(
+            src_ref=packed,
+            dst_ref=slots.at[source_u, lax.rem(source_v - target_v + 1 + n_patch, n_patch)],
+            send_sem=all_send.at[i],
+            recv_sem=all_recv.at[i],
+            device_id={"dir": u, "patch": v},
+            device_id_type=MESH,
+        )
+
+    loop(n_all - 1, lambda i: gather(i, False).start())
+    loop(n_all - 1, lambda i: gather(i, False).wait_send())
+    loop(n_all - 1, lambda i: gather(i, True).wait_recv())
+
+    x_v = copies([(slab_x.at[0, mid], slab_x.at[(-b) % 3, mid], 0, b) for b in (1, -1)]
+                 + [(strip_x.at[1], slab_far.at[0, mid], 0, 2), (strip_x.at[0], slab_far.at[1, mid], 0, -2)], number(4))
+    x_u = []
+    for b in range(3):
+        x_u += slab_items(slab_x, b, (1, -1, 2, -2))
+    for b in range(2):
+        x_u += slab_items(slab_far, b, (1, -1, 2, -2))
+    x_u = copies(x_u, number(len(x_u)))
+
     start(x_v)
-    start(far_first)
 
     low = lax.broadcasted_iota(jnp.int32, (cv, 128), 1) < 64
     for d in range(n_dir):
@@ -711,7 +732,8 @@
     def second_leg():
         received(x_v)
         start(x_u)
-        received([far_first[0], far_first[1], far_first[4], far_first[5]])
+        received(x_far[:2])
+        received(f_far[:2])
         start(far_second)
 
     coarse_cycle((cu * n_dir, cv * n_patch // 2), load2, tables, coarse, second_leg)
@@ -761,13 +783,14 @@
     sweep(*level1, U1 - 12, mu + 24, window1(12))
     sweep(*level1, U1 - 9, mu + 18, window1(9))
     sweep(*level1, U1 - 6, mu + 12, window1(6))
-    received([far_first[k] for k in (2, 3, 6, 7)])
+    received(x_far[2:])
+    received(f_far[2:])
     received(far_second)
     for x, halo in ((x0, xh), (f0, fh)):
         lay_sides(x, FAR, halo.far_v, halo.reach, halo.near)
         lay_sides(x, halo.near, halo.near_v, halo.reach)
         lay_ups(x, FAR, halo.far_u, halo.near)
-    for made in (masks, f_near, x_near, f_v, f_u, x_v, x_u, far_first, far_second):
+    for made in (masks, f_near, x_near, f_v, f_u, x_v, x_u, x_far, f_far, far_second):
         sent(made)
     prolong(lambda i, k: x1[0, U1 - (U0 + 1) // 2 + i, k : k + span], 16, up0, x0, s0)
     level0 = (x0, s0, f0, d0, e0, band0)
@@ -787,15 +810,15 @@
     eu, eq = gu // 2, up8(gh // 4)
     rows0, cols0, rows1, cols1 = nu + 18, nv + 32, mu + 30, up8(mv + 37)
     operands = [right_side, guess, jnp.transpose(mask_fine, (0, 2, 1)), jnp.transpose(mask_next, (0, 2, 1))]
-    operands += [jnp.asarray(t) for t in fine_weights(nw)]
-    operands += [jnp.asarray(t) for t in coarse_weights(nw)]
     operands += [jnp.asarray(np.eye(nv, 128, dtype=np.float32))]
-    operands += [jnp.asarray(spots(nv, 16, cols0, 32, 9)[:, :]), jnp.asarray(spots(mv, 22, cols1, 16, 15))]
+    operands += [jnp.asarray(spots(nv, 16, cols0, 32, 9)), jnp.asarray(spots(mv, mv + 10, cols1, 16, mu + 3))]
+    operands += [jnp.asarray(t) for t in fine_weights(nw) + coarse_weights(nw)]
 
     def vmem(*shape):
         return pltpu.VMEM(shape, jnp.float32)
 
-    scratch = [vmem(planes, rows0, cols0, 128)] * 3 + [vmem(planes, rows0, nv + 16, 128)] * 2
+    scratch = [pltpu.VMEM(t.shape, t.dtype) for t in operands]
+    scratch += [vmem(planes, rows0, cols0, 128)] * 3 + [vmem(planes, rows0, nv + 16, 128)] * 2
     scratch += [vmem(1, rows1, cols1, 128)] * 3 + [vmem(1, rows1, cols1 - 16, 128)] * 2
     scratch += [vmem(nu + 4, nv + 16, 128), vmem(mu + 4, cols1 - 16, 128), vmem(mu, nv + 16, 128)]
     scratch += [vmem(24, cols1, 128), vmem(planes, 24, cols1, 128)]
@@ -809,12 +832,13 @@
     scratch += [vmem(gu + 4, gh + 16, 128), vmem(gu, gh, 128), vmem(eu, eq + 16, 128), vmem(eu, eq, 128)]
     scratch += [vmem(eu + 6, eq, 128), vmem(eu + 6, eq, 128), vmem(eu, gh + 16, 128)]
     scratch += [pltpu.SemaphoreType.DMA((160,))] * 2 + [pltpu.SemaphoreType.DMA((n_dir * n_patch - 1,))] * 2
-    space = pl.BlockSpec(memory_space=pltpu.VMEM)
+    scratch += [pltpu.SemaphoreType.DMA((len(operands),))]
+    space = pl.BlockSpec(memory_space=pltpu.MemorySpace.HBM)
     return pl.pallas_call(
         functools.partial(kernel, (n_dir, n_patch, nu, nv, planes)),
         out_shape=jax.ShapeDtypeStruct(right_side.shape, jnp.float32),
         in_specs=[space] * len(operands),
-        out_specs=space,
+        out_specs=pl.BlockSpec(memory_space=pltpu.VMEM),
         scratch_shapes=scratch,
         compiler_params=pltpu.CompilerParams(
             collective_id=0, has_side_effects=True, vmem_limit_bytes=60 * 2**20

time: 111 us -> 103 us (0.928)
  Pallas kernels: 109 us -> 101 us
    pallas_call x1, Pallas kernels: 109 us -> 101 us  [on_device(): pl.pallas_call(functools.partial(kernel, (n_dir, n_patch, nu, nv, planes)...]
where the time goes in v3:
time: 103 us
  Pallas kernels  101 us (98%)
  local copies, waits for them, and re-layouts  1.92 us (2%)
    pallas_call x1, Pallas kernels, on_device(): pl.pallas_call(functools.partial(kernel, (n_dir, n_patch, nu, nv, planes)...  101 us

profile of v3, /device:TPU:0, one launch (start us, length us, event | category | flops | bytes accessed | tf_op | source)
XLA Modules:
  0.0 102.8 jit_solution(16683223682620095912)
XLA Ops:
  0.0 100.8 %vcycle.1 = f32[24,24,256]{2,1,0:T(8,128)} custom-call(f32[24,24,256]{2,1,0:T(8,128)} %refs_0_.1, f32[24,24,256]{2,1,0:T(8,128)} %refs_1_.1, s32[24,2,24]{2,1,0:T(2,128)} %bitcast.2, s32[12,1,12]{2,1,0:T(1,128)} %bitcast.3, f32[24,128]{1,0:T(8,128)} %constant.24.clone.refs_4_, f32[56,128]{1,0:T(8,128)} %constant.25.clone.refs_5_, ...), custom_call_target="tpu_custom_call" | custom-call | tf_op jit(solution)/shard_map/vcycle/pallas_call | solution.py:837
  100.8 1.9 %copy.18 = f32[24,24,256]{2,1,0:T(8,128)} copy(f32[24,24,256]{2,1,0:T(8,128)} %vcycle.1) | data formatting | bytes 1179648

commit v4 on v3

--- a/solution.py
+++ b/solution.py
@@ -15,7 +15,8 @@
 OMEGA = 0.5
 MESH = pl.DeviceIdType.MESH
 AROUND = ((0, 1), (0, -1), (1, 0), (-1, 0), (1, 1), (1, -1), (-1, 1), (-1, -1))
-BASIS = (2496, 1176, 96)
+FIVE = (0, 192, 2352, 4992, 2352, 192, 0)
+STIFF = (-3, -72, -45, 240, -45, -72, -3)
 KAPPA = OMEGA * 42 / 5040.0**3
 FAR = 4
 
@@ -45,8 +46,8 @@
     tables = []
     for n in (wide, narrow):
         copies = np.eye(128 // n, dtype=np.float32)
-        five = band(n, n, (0, 96, 1176, 2496, 1176, 96, 0))
-        stiff = band(n, n, (-1, -24, -15, 80, -15, -24, -1))
+        five = band(n, n, FIVE)
+        stiff = band(n, n, STIFF)
         tables.append(np.stack([np.kron(copies, five), np.kron(copies, stiff)]))
     move = subdivision(narrow, wide, narrow)
     halves = np.eye(128 // wide, dtype=np.float32)
@@ -71,26 +72,17 @@
     return x[3], x[2] + x[4], x[1] + x[5], x[0] + x[6]
 
 
-def five_taps(s):
-    return BASIS[0] * s[0] + BASIS[1] * s[1] + BASIS[2] * s[2]
-
-
-def stiff_taps(s):
-    return 80.0 * s[0] - 15.0 * s[1] - 24.0 * s[2] - s[3]
-
-
 def first_pass(x):
     s = sums(x)
-    d, e = 2 * KAPPA * s[3], 3 * KAPPA * s[3]
-    for k, (p, q) in enumerate(((2336, 4752), (1206, 2397), (144, 264))):
-        d, e = d + p * KAPPA * s[k], e + q * KAPPA * s[k]
+    d = s[3] + 72.0 * s[2] + 603.0 * s[1] + 1168.0 * s[0]
+    e = s[3] + 88.0 * s[2] + 799.0 * s[1] + 1584.0 * s[0]
     return d, e
 
 
 def second_pass(d, e):
     d, e = sums(d), sums(e)
-    g = five_taps(e) - (4912.0 * d[0] + 2367.0 * d[1] + 216.0 * d[2] + d[3])
-    q = five_taps(d) - stiff_taps(e)
+    g = (3744.0 * e[0] + 1764.0 * e[1] + 144.0 * e[2]) - (4912.0 * d[0] + 2367.0 * d[1] + 216.0 * d[2] + d[3])
+    q = (1664.0 * d[0] + 784.0 * d[1] + 64.0 * d[2]) - (80.0 * e[0] - 15.0 * e[1] - 24.0 * e[2] - e[3])
     return g, q
 
 
@@ -111,7 +103,7 @@
 def rows_at_once(count, rows):
     best = 1
     for n in range(1, count + 1):
-        if count % n == 0 and n * rows <= 240:
+        if count % n == 0 and n * rows <= 600:
             best = n
     return best
 
@@ -126,7 +118,7 @@
     def one(u):
         d[u + 3], e[u + 3] = first_pass([x[at + u, base - 3 + k : base - 3 + k + rows, :] for k in range(7)])
 
-    loop(count, one, 3)
+    loop(count, one, 8)
     size = rows_at_once(count, rows)
 
     def some(i):
@@ -163,7 +155,7 @@
 
     def smooth2():
         def use(u, value):
-            put2(u, x2[edge + u, 8 : 8 + nh] + ((OMEGA / 4) * load2[u] - value))
+            put2(u, x2[edge + u, 8 : 8 + nh] + ((OMEGA / 4) * load2[u] - KAPPA * value))
         apply_packed(x2, d2, e2, tables[0], edge, 8, nh, nu, use)
 
     loop(nu, lambda u: put2(u, (OMEGA / 4) * load2[u]), 4)
@@ -172,7 +164,7 @@
     size = rows_at_once(nu, nh)
 
     def keep(u, value):
-        t2[u] = load2[u] - 8.0 * value
+        t2[u] = load2[u] - (8 * KAPPA) * value
 
     apply_packed(x2, d2, e2, tables[0], edge, 8, nh, nu, keep)
 
@@ -208,7 +200,7 @@
 
     def smooth3(i):
         def use(u, value):
-            put3(u, x3[u, 8 : 8 + nqp] + ((OMEGA / 8) * f3[u] - value))
+            put3(u, x3[u, 8 : 8 + nqp] + ((OMEGA / 8) * f3[u] - KAPPA * value))
         apply_packed(x3, d3, e3, tables[1], 0, 8, nqp, cu, use)
 
     loop(2 * SWEEPS - 1, smooth3)
@@ -244,8 +236,8 @@
 def fine_weights(width):
     tables = []
     for n in (width, width // 2):
-        five = band(n, n, (0, 96, 1176, 2496, 1176, 96, 0))
-        stiff = band(n, n, (-1, -24, -15, 80, -15, -24, -1))
+        five = band(n, n, FIVE)
+        stiff = band(n, n, STIFF)
         move = subdivision(n // 2, n, max(n // 2, 128))
         tables += [np.stack([five, stiff]), move, np.ascontiguousarray(move.T)]
     return [t.astype(jnp.bfloat16) for t in tables]
@@ -279,8 +271,8 @@
     sources, out, held, refs = refs[:16], refs[16], refs[17:33], refs[33:]
     rs, guess, mask0, mask1, pick, pick0, pick1, band0, down0, up0, band1, down1, up1 = held[:13]
     tables = held[13:]
-    x0, s0, f0, d0, e0, x1, s1, f1, d1, e1, r1, r2, t1, tv, tw = refs[:15]
-    refs = refs[15:]
+    x0, s0, f0, d0, e0, x1, s1, f1, d1, e1, r1, r2, t1, tv, tw, du, eu = refs[:17]
+    refs = refs[17:]
     side_send, side_recv, up_recv = refs[:3]
     xh, fh = Halo(refs[3:9], 5), Halo(refs[9:15], 2)
     lines0, lines1, line0, line1 = refs[15:19]
@@ -342,6 +334,11 @@
     def greet(i):
         u, v = place(lax.rem(me + 1 + i, n_all))
         pl.semaphore_signal(barrier, inc=1, device_id={"dir": u, "patch": v}, device_id_type=MESH)
+
+    for flag, rows in ((me_u == 0, slice(0, 3)), (me_u == n_dir - 1, slice(nu + 3, nu + 6))):
+        @pl.when(flag)
+        def _():
+            side_recv[:, :, :, rows] = jnp.zeros((SWEEPS, 2, planes, 3, 3, 128), jnp.float32)
 
     loop(n_all - 1, greet)
     loads = [pltpu.make_async_copy(source, to, load_sem.at[k]) for k, (source, to) in enumerate(zip(sources, held))]
@@ -379,7 +376,7 @@
                 lanes = slice(w * 128, w * 128 + 128)
                 x0[w, U0 + u, V0 : V0 + nv] = m * guess[u, :, lanes]
                 f0[w, U0 + u, V0 : V0 + nv] = OMEGA * m * rs[u, :, lanes]
-                s0[w, U0 + u, V0 : V0 + nv] = m
+                s0[w, U0 + u, V0 : V0 + nv] = KAPPA * m
 
     loop(nu // 4, own)
 
@@ -430,7 +427,7 @@
                             else:
                                 line = line + lines0[0, u + j, w : w + 1, :]
                             marks.append(spread(pick0[...], line))
-                    full = mul(jnp.concatenate(marks, axis=0), ones)
+                    full = KAPPA * mul(jnp.concatenate(marks, axis=0), ones)
                     n0 = s0.shape[2]
                     for w in range(planes):
                         for j in range(3):
@@ -448,7 +445,7 @@
                         for b in range(1, 5):
                             line = line + lines1[b, u]
                         marks.append(spread(pick1[...], line))
-                    full = mul(jnp.concatenate(marks, axis=0), ones)
+                    full = KAPPA * mul(jnp.concatenate(marks, axis=0), ones)
                     n1 = s1.shape[2]
                     for j in range(3):
                         s1[0, to.start + 3 * i + j] = full[j * n1 : (j + 1) * n1]
@@ -465,7 +462,7 @@
                 t = [x[w, u, lo - 3 + k : lo - 3 + k + size, :] for k in range(7)]
                 d[w, u, 0:size], e[w, u, 0:size] = first_pass(t)
 
-        loop(count + 6, one, 3)
+        loop(count + 6, one, 6)
         rows = rows_at_once(count, size)
 
         def some(i):
@@ -588,12 +585,32 @@
     ff, fs = far_items(f0, fh)
     x_far, f_far = copies(xf, number(4)), copies(ff, number(4))
     far_second = copies(xs + fs, number(16))
+    def sweep_tiles(tiles, send):
+        gs, qs = [], []
+        for w in range(planes):
+            both = [second_pass([du[w, u, 8 * t + 5 + k : 8 * t + 13 + k] for k in range(7)],
+                                [eu[w, u, 8 * t + 5 + k : 8 * t + 13 + k] for k in range(7)])
+                    for u in range(nu) for t in tiles]
+            gs.append(jnp.concatenate([g for g, _ in both], axis=0))
+            qs.append(jnp.concatenate([q for _, q in both], axis=0))
+        value = last_pass(jnp.concatenate(gs, axis=1), jnp.concatenate(qs, axis=1), band0)
+        for u in range(nu):
+            for n, t in enumerate(tiles):
+                for w in range(planes):
+                    r = (u * len(tiles) + n) * 8
+                    at = (w, U0 + u, slice(V0 + 8 * t, V0 + 8 * t + 8))
+                    new = x0[at] + (f0[at] - s0[at] * value[r : r + 8, w * 128 : (w + 1) * 128])
+                    x0[at] = new
+                    if t == 0:
+                        send[0, w, u] = new[0:3]
+                    if t == nv // 8 - 1:
+                        send[1, w, u] = new[5:8]
+
     base = number(8 * SWEEPS)
     f_near = copies(near_items(f0, fh.near, fh.send_near, fh.near_v, fh.near_u), number(8))
     block0 = (V0, nv)
 
     def smooth0(i):
-        stage(x0, 3, side_send.at[i])
         made = copies(near_items(x0, 3, side_send.at[i], side_recv.at[i], up_recv.at[i]), base + 8 * i)
         start(made)
 
@@ -605,12 +622,32 @@
             prepare()
 
         pl.when(i == 1)(expand)
-        received(made)
-        sent(made)
-        lay_sides(x0, 3, side_recv.at[i], 3)
+        received(made[2:4])
         lay_ups(x0, 3, up_recv.at[i])
-        sweep(x0, s0, f0, d0, e0, band0, U0, nu, block0)
-
+
+        def own_columns(u):
+            for w in range(planes):
+                d, e = first_pass([x0[w, U0 + u - 3 + k, V0 : V0 + nv] for k in range(7)])
+                du[w, u, 8 : 8 + nv], eu[w, u, 8 : 8 + nv] = d, e
+
+        loop(nu, own_columns, 6)
+        sent(made[2:4])
+        sweep_tiles(range(1, nv // 8 - 1), side_send.at[i + 1])
+        received(made[:2])
+        received(made[4:])
+
+        def side_columns(u):
+            for w in range(planes):
+                for s, at in ((0, 5), (1, 8 + nv)):
+                    d, e = first_pass([side_recv[i, s, w, u + k] for k in range(7)])
+                    du[w, u, at : at + 3], eu[w, u, at : at + 3] = d, e
+
+        loop(nu, side_columns, 6)
+        sent(made[:2])
+        sent(made[4:])
+        sweep_tiles((0, nv // 8 - 1), side_send.at[i + 1])
+
+    stage(x0, 3, side_send.at[0])
     loop(SWEEPS, smooth0)
 
     stage(x0, xh.near, xh.send_near)
@@ -630,7 +667,7 @@
     mid = slice(U1, U1 + mu)
 
     def load1(i):
-        line = (OMEGA / 2) * s1[0, U1 + i, V1 : V1 + mv] * restrict(r1, i, wide[1], V0 - wide[0] - 2, mv)
+        line = (OMEGA / 2 / KAPPA) * s1[0, U1 + i, V1 : V1 + mv] * restrict(r1, i, wide[1], V0 - wide[0] - 2, mv)
         slab_f[0, U1 + i] = line
 
     loop(mu, load1, 4)
@@ -762,7 +799,7 @@
                 p, q, r = tw[w, t], tw[w, t + 1], tw[w, t + 2]
                 for j, y in enumerate((0.5 * (p + q), 0.125 * (p + r) + 0.75 * q)):
                     u = 2 * t + j
-                    x[w, u] = x[w, u] + jnp.where(s[w, u] > 0.5, y, 0.0)
+                    x[w, u] = x[w, u] + jnp.where(s[w, u] > 0.0, y, 0.0)
 
         loop(21, add)
 
@@ -821,8 +858,8 @@
     scratch += [vmem(planes, rows0, cols0, 128)] * 3 + [vmem(planes, rows0, nv + 16, 128)] * 2
     scratch += [vmem(1, rows1, cols1, 128)] * 3 + [vmem(1, rows1, cols1 - 16, 128)] * 2
     scratch += [vmem(nu + 4, nv + 16, 128), vmem(mu + 4, cols1 - 16, 128), vmem(mu, nv + 16, 128)]
-    scratch += [vmem(24, cols1, 128), vmem(planes, 24, cols1, 128)]
-    scratch += [vmem(SWEEPS, 2, planes, nu, 3, 128), vmem(SWEEPS, 2, planes, nu + 6, 3, 128)]
+    scratch += [vmem(24, cols1, 128), vmem(planes, 24, cols1, 128)] + [vmem(planes, nu, nv + 16, 128)] * 2
+    scratch += [vmem(SWEEPS + 1, 2, planes, nu, 3, 128), vmem(SWEEPS, 2, planes, nu + 6, 3, 128)]
     scratch += [vmem(SWEEPS, 2, planes, 3, nv, 128)]
     scratch += Halo.scratch(planes, nu, nv, 5) + Halo.scratch(planes, nu, nv, 2)
     scratch += [vmem(3, rows0, planes, 128), vmem(5, rows1, 1, 128), vmem(3, nu, planes, 128), vmem(5, mu, 1, 128)]

time: 103 us -> 95.1 us (0.923)
  Pallas kernels: 101 us -> 92.9 us
    pallas_call x1, Pallas kernels: 101 us -> 92.9 us  [on_device(): pl.pallas_call(functools.partial(kernel, (n_dir, n_patch, nu, nv, planes)...]
where the time goes in v4:
time: 95.1 us; the launch traced here: 94.9 us
  Pallas kernels  92.9 us (98%)
  local copies, waits for them, and re-layouts  1.92 us (2%)
    pallas_call x1, Pallas kernels, on_device(): pl.pallas_call(functools.partial(kernel, (n_dir, n_patch, nu, nv, planes)...  92.9 us
    unnamed x1, local copies, waits for them, and re-layouts  1.92 us

profile of v4, /device:TPU:0, one launch (start us, length us, event | category | flops | bytes accessed | tf_op | source)
XLA Modules:
  0.0 94.9 jit_solution(14572743526347277733)
XLA Ops:
  0.0 92.9 %vcycle.1 = f32[24,24,256]{2,1,0:T(8,128)} custom-call(f32[24,24,256]{2,1,0:T(8,128)} %refs_0_.1, f32[24,24,256]{2,1,0:T(8,128)} %refs_1_.1, s32[24,2,24]{2,1,0:T(2,128)} %bitcast.2, s32[12,1,12]{2,1,0:T(1,128)} %bitcast.3, f32[24,128]{1,0:T(8,128)} %constant.24.clone.refs_4_, f32[56,128]{1,0:T(8,128)} %constant.25.clone.refs_5_, ...), custom_call_target="tpu_custom_call" | custom-call | tf_op jit(solution)/shard_map/vcycle/pallas_call | solution.py:874
  93.0 1.9 %copy.18 = f32[24,24,256]{2,1,0:T(8,128)} copy(f32[24,24,256]{2,1,0:T(8,128)} %vcycle.1) | data formatting | bytes 1179648

commit v5 on v4

--- a/solution.py
+++ b/solution.py
@@ -195,7 +195,7 @@
             lines.append(line)
         f3[i, 0:nq] = jnp.where(first, lines[0], lines[1])
 
-    loop(cu, restrict, 4)
+    loop(cu, restrict, 12)
     loop(cu, lambda u: put3(u, (OMEGA / 8) * f3[u]), 4)
 
     def smooth3(i):
@@ -544,7 +544,7 @@
             for w in range(planes):
                 strips[0, w, u] = x[w, U0 + u, V0 + skip : V0 + skip + h]
                 strips[1, w, u] = x[w, U0 + u, V0 + nv - skip - h : V0 + nv - skip]
-        loop(nu, one, 4)
+        loop(nu, one, 12)
 
     def lay_sides(x, h, sides, reach, skip=0, extra=None):
         extra = reach if extra is None else extra
@@ -555,7 +555,7 @@
                     for w in range(planes):
                         x[w, u, V0 - skip - h : V0 - skip] = sides[0, w, u - U0 + reach]
                         x[w, u, V0 + nv + skip : V0 + nv + skip + h] = sides[1, w, u - U0 + reach]
-                loop(n, one, 4)
+                loop(n, one, 9)
             given(present(a), body)
 
     def lay_ups(x, h, ups, skip=0):
@@ -630,7 +630,7 @@
                 d, e = first_pass([x0[w, U0 + u - 3 + k, V0 : V0 + nv] for k in range(7)])
                 du[w, u, 8 : 8 + nv], eu[w, u, 8 : 8 + nv] = d, e
 
-        loop(nu, own_columns, 6)
+        loop(nu, own_columns, 12)
         sent(made[2:4])
         sweep_tiles(range(1, nv // 8 - 1), side_send.at[i + 1])
         received(made[:2])
@@ -642,7 +642,7 @@
                     d, e = first_pass([side_recv[i, s, w, u + k] for k in range(7)])
                     du[w, u, at : at + 3], eu[w, u, at : at + 3] = d, e
 
-        loop(nu, side_columns, 6)
+        loop(nu, side_columns, 12)
         sent(made[:2])
         sent(made[4:])
         sweep_tiles((0, nv // 8 - 1), side_send.at[i + 1])
@@ -670,7 +670,7 @@
         line = (OMEGA / 2 / KAPPA) * s1[0, U1 + i, V1 : V1 + mv] * restrict(r1, i, wide[1], V0 - wide[0] - 2, mv)
         slab_f[0, U1 + i] = line
 
-    loop(mu, load1, 4)
+    loop(mu, load1, 12)
 
     def slab_items(slab, b_from, steps):
         items = []
@@ -698,7 +698,7 @@
                     for x in targets:
                         for b in (-1, 0, 1):
                             x[0, u, V1 + b * mv : V1 + (b + 1) * mv] = slab[b % 3, u]
-                loop(to.stop - to.start, one, 3)
+                loop(to.stop - to.start, one, 6)
             given(present(a), body)
 
     lay_slab(slab_f, (f1, x1), (0, -1, 1))
@@ -716,14 +716,14 @@
         strip_x[0, u] = x1[0, U1 + u, V1 : V1 + 3]
         strip_x[1, u] = x1[0, U1 + u, V1 + mv - 3 : V1 + mv]
 
-    loop(mu, own_x1, 3)
+    loop(mu, own_x1, 12)
     at1 = window1(2)
     residual(*level1, down1, 4.0, U1 - 2, mu + 4, at1, r2)
 
     def load_2(i):
         c2[i, 0:cv] = restrict(r2, i, at1[1], V1 - at1[0] - 2, cv)
 
-    loop(cu, load_2, 3)
+    loop(cu, load_2, 6)
 
     half = cu // 2
     for j in range(half):
@@ -783,16 +783,16 @@
             tv[i, pl.ds(6, span, stride=2), :] = 0.125 * (b + a) + 0.75 * h
             tv[i, pl.ds(7, span, stride=2), :] = 0.5 * (h + a)
 
-        loop(24, one, 3)
+        loop(24, one, 8)
         n = tv.shape[1]
 
         def widen(i):
-            y = split_mul(tv[pl.ds(4 * i, 4)].reshape(4 * n, 128), table[...])
+            y = split_mul(tv[pl.ds(8 * i, 8)].reshape(8 * n, 128), table[...])
             for w in range(x.shape[0]):
-                for j in range(4):
-                    tw[w, 4 * i + j] = y[j * n : (j + 1) * n, w * 128 : (w + 1) * 128]
-
-        loop(6, widen)
+                for j in range(8):
+                    tw[w, 8 * i + j] = y[j * n : (j + 1) * n, w * 128 : (w + 1) * 128]
+
+        loop(3, widen)
 
         def add(t):
             for w in range(x.shape[0]):
@@ -801,7 +801,7 @@
                     u = 2 * t + j
                     x[w, u] = x[w, u] + jnp.where(s[w, u] > 0.0, y, 0.0)
 
-        loop(21, add)
+        loop(21, add, 3)
 
     received(x_u)
     lay_slab(slab_x, (x1,), (0, -1, 1, -2, 2))

time: 95.1 us -> 93.7 us (0.985)
  Pallas kernels: 92.9 us -> 91.6 us
    pallas_call x1, Pallas kernels: 92.9 us -> 91.6 us  [on_device(): pl.pallas_call(functools.partial(kernel, (n_dir, n_patch, nu, nv, planes)...]
where the time goes in v5:
time: 93.7 us; the launch traced here: 93.5 us
  Pallas kernels  91.6 us (98%)
  local copies, waits for them, and re-layouts  1.92 us (2%)
    pallas_call x1, Pallas kernels, on_device(): pl.pallas_call(functools.partial(kernel, (n_dir, n_patch, nu, nv, planes)...  91.6 us
    unnamed x1, local copies, waits for them, and re-layouts  1.92 us

profile of v5, /device:TPU:0, one launch (start us, length us, event | category | flops | bytes accessed | tf_op | source)
XLA Modules:
  0.0 93.5 jit_solution(4085675458556574528)
XLA Ops:
  0.0 91.6 %vcycle.1 = f32[24,24,256]{2,1,0:T(8,128)} custom-call(f32[24,24,256]{2,1,0:T(8,128)} %refs_0_.1, f32[24,24,256]{2,1,0:T(8,128)} %refs_1_.1, s32[24,2,24]{2,1,0:T(2,128)} %bitcast.2, s32[12,1,12]{2,1,0:T(1,128)} %bitcast.3, f32[24,128]{1,0:T(8,128)} %constant.24.clone.refs_4_, f32[56,128]{1,0:T(8,128)} %constant.25.clone.refs_5_, ...), custom_call_target="tpu_custom_call" | custom-call | tf_op jit(solution)/shard_map/vcycle/pallas_call | solution.py:874
  91.6 1.9 %copy.18 = f32[24,24,256]{2,1,0:T(8,128)} copy(f32[24,24,256]{2,1,0:T(8,128)} %vcycle.1) | data formatting | bytes 1179648

commit v6 on v5

--- a/solution.py
+++ b/solution.py
@@ -118,7 +118,7 @@
     def one(u):
         d[u + 3], e[u + 3] = first_pass([x[at + u, base - 3 + k : base - 3 + k + rows, :] for k in range(7)])
 
-    loop(count, one, 8)
+    loop(count, one, 12)
     size = rows_at_once(count, rows)
 
     def some(i):
@@ -462,7 +462,7 @@
                 t = [x[w, u, lo - 3 + k : lo - 3 + k + size, :] for k in range(7)]
                 d[w, u, 0:size], e[w, u, 0:size] = first_pass(t)
 
-        loop(count + 6, one, 6)
+        loop(count + 6, one, 12)
         rows = rows_at_once(count, size)
 
         def some(i):

time: 93.7 us -> 93.5 us (level)
  no operation moved by 1% of the time
where the time goes in v6:
time: 93.5 us; the launch traced here: 93.3 us
  Pallas kernels  91.4 us (98%)
  local copies, waits for them, and re-layouts  1.92 us (2%)
    pallas_call x1, Pallas kernels, on_device(): pl.pallas_call(functools.partial(kernel, (n_dir, n_patch, nu, nv, planes)...  91.4 us
    unnamed x1, local copies, waits for them, and re-layouts  1.92 us

profile of v6, /device:TPU:0, one launch (start us, length us, event | category | flops | bytes accessed | tf_op | source)
XLA Modules:
  0.0 93.3 jit_solution(86356257011154192)
XLA Ops:
  0.0 91.4 %vcycle.1 = f32[24,24,256]{2,1,0:T(8,128)} custom-call(f32[24,24,256]{2,1,0:T(8,128)} %refs_0_.1, f32[24,24,256]{2,1,0:T(8,128)} %refs_1_.1, s32[24,2,24]{2,1,0:T(2,128)} %bitcast.2, s32[12,1,12]{2,1,0:T(1,128)} %bitcast.3, f32[24,128]{1,0:T(8,128)} %constant.24.clone.refs_4_, f32[56,128]{1,0:T(8,128)} %constant.25.clone.refs_5_, ...), custom_call_target="tpu_custom_call" | custom-call | tf_op jit(solution)/shard_map/vcycle/pallas_call | solution.py:874
  91.4 1.9 %copy.18 = f32[24,24,256]{2,1,0:T(8,128)} copy(f32[24,24,256]{2,1,0:T(8,128)} %vcycle.1) | data formatting | bytes 1179648
